TPU v7x, 256 devices: a whole 4x4x8 slice. The times are simulated.
256 devices in a mesh: wide: 32 (over z, x), narrow: 8 (over y, core).
Axes of the slice: x: 4, y: 4, z: 8, core: 2. Of those that a mesh axis runs over, the one named last changes fastest.
Arguments:
- payload: bfloat16 [1048576, 128], P(('wide', 'narrow')), may hold values from -6 to 6
- first_key: int32 [1048576], P(('wide', 'narrow')), may hold values from 0 to 1073741823
- second_key: int32 [1048576], P(('wide', 'narrow')), may hold values from 0 to 1073741823
- live: int32 [1048576], P(('wide', 'narrow')), may hold values from 0 to 1
- first_bucket: int32 [1048576], P(('wide', 'narrow')), may hold values from 0 to 31, as said below
- second_bucket: int32 [1048576], P(('wide', 'narrow')), may hold values from 0 to 7
Outputs:
- group_mean: bfloat16 [1048576, 128], P(('wide', 'narrow'))
- duplicate_count: int32 [], replicated
Inputs may be any that keep to these rules, and one draw needn't show every extreme that they name: Each device's rows name each pair (first_bucket, second_bucket) exactly 16 times; in every draw there is one bucket pair all of whose rows survive; other rows survive or not as `live` says.
All inputs are finite; a program needn't handle non-finite values.
Results may differ from a plain program's by a relative error of at most 0.001.
Values may be sent and summed in bfloat16 or wider, within the bound.
A program may use at most 64 MiB of HBM per device.

v0:
```python
import jax
import jax.numpy as jnp
from jax import lax
from jax.sharding import Mesh
from jax.sharding import PartitionSpec as P

WIDE = ("wide_0", "wide_1")
NARROW = ("narrow_0", "narrow_1")
WIDE_NARROW = ("wide_0", "wide_1", "narrow_0", "narrow_1")


def in_blocks(array, dim, length):
    lengths = array.shape
    pieces = array.reshape(*lengths[:dim], length, lengths[dim] // length, *lengths[dim + 1 :])
    return jnp.moveaxis(pieces, dim, 0)


def joined_along(pieces, dim):
    lengths = list(pieces.shape[1:])
    lengths[dim] *= pieces.shape[0]
    return jnp.moveaxis(pieces, 0, dim).reshape(lengths)


def joined_exchange(array, axis, axes, splits, concats):
    sizes = [lax.axis_size(a) for a in axes]
    pieces = in_blocks(array, splits[0], sizes[0])
    pieces = jnp.moveaxis(in_blocks(pieces, splits[1] + 1, sizes[1]), 0, 1)
    inside = pieces.shape[2:]
    pieces = pieces.reshape(-1, *inside)
    pieces = lax.all_to_all(pieces, axis, split_axis=0, concat_axis=0, tiled=True)
    pieces = joined_along(pieces.reshape(*sizes, *inside), concats[0] + 1)
    return joined_along(pieces, concats[1])


def by_axis(array, axes):
    for axis in axes:
        array = lax.psum(array, axis)
    return array


def pair_mask(row_one, row_two, row_live, col_one, col_two, col_live):
    return (
        (row_one[:, None] == col_one[None, :])
        & (row_two[:, None] == col_two[None, :])
        & (row_live[:, None] > 0)
        & (col_live[None, :] > 0)
    )


def on_device(payload, first_key, second_key, live, first_bucket, second_bucket):
    wide_count = lax.axis_size(WIDE)
    narrow_count = lax.axis_size(NARROW)
    row_count, feature_cols = payload.shape
    slot_rows = row_count // (wide_count * narrow_count)
    owner = first_bucket * narrow_count + second_bucket
    sort_order = jnp.argsort(owner, stable=True)
    inverse = jnp.argsort(sort_order, stable=True)
    sent_rows = payload[sort_order].reshape(wide_count, narrow_count, slot_rows, feature_cols)
    shaped = (wide_count, narrow_count, slot_rows)
    tags = jnp.stack(
        [
            first_key[sort_order].reshape(shaped),
            second_key[sort_order].reshape(shaped),
            live[sort_order].reshape(shaped),
        ],
        axis=2,
    )
    got_rows, got_tags = (
        joined_exchange(sent_rows, WIDE_NARROW, (WIDE, NARROW), (0, 1), (0, 1)),
        joined_exchange(tags, WIDE_NARROW, (WIDE, NARROW), (0, 1), (0, 1)),
    )
    owner_rows = wide_count * narrow_count * slot_rows
    flat_rows = got_rows.reshape(owner_rows, feature_cols)
    keys_one = got_tags[:, :, 0, :].reshape(owner_rows)
    keys_two = got_tags[:, :, 1, :].reshape(owner_rows)
    alive = got_tags[:, :, 2, :].reshape(owner_rows)
    tile_rows = min(512, owner_rows)
    column_pos = lax.iota(jnp.int32, owner_rows)

    def full_block(block_index, running):
        group_means, duplicate_total = running
        block_start = block_index * tile_rows
        row_one = lax.dynamic_slice_in_dim(keys_one, block_start, tile_rows)
        row_two = lax.dynamic_slice_in_dim(keys_two, block_start, tile_rows)
        row_live = lax.dynamic_slice_in_dim(alive, block_start, tile_rows)
        same = pair_mask(row_one, row_two, row_live, keys_one, keys_two, alive)
        sums = jnp.dot(same.astype(jnp.bfloat16), flat_rows, preferred_element_type=jnp.float32)
        counts = jnp.sum(same.astype(jnp.float32), axis=1)
        row_pos = block_start + lax.iota(jnp.int32, tile_rows)
        earlier = same & (column_pos[None, :] < row_pos[:, None])
        duplicate_total = duplicate_total + jnp.sum(jnp.any(earlier, axis=1).astype(jnp.float32))
        block_mean = (sums / jnp.maximum(counts, 1.0)[:, None]).astype(jnp.bfloat16)
        group_means = lax.dynamic_update_slice_in_dim(group_means, block_mean, block_start, 0)
        return (group_means, duplicate_total)

    start_state = (jnp.zeros((owner_rows, feature_cols), jnp.bfloat16), jnp.zeros((), jnp.float32))
    group_means, duplicate_total = lax.fori_loop(
        0, owner_rows // tile_rows, full_block, start_state
    )
    back_rows = group_means.reshape(wide_count, narrow_count, slot_rows, feature_cols)
    returned = joined_exchange(back_rows, WIDE_NARROW, (WIDE, NARROW), (0, 1), (0, 1))
    group_mean = returned.reshape(row_count, feature_cols)[inverse]
    overall = by_axis(duplicate_total, WIDE_NARROW)
    return (group_mean, overall.astype(jnp.int32))


def solution(mesh):
    torus = Mesh(mesh.devices.reshape(8, 4, 4, 2), ("wide_0", "wide_1", "narrow_0", "narrow_1"))
    return jax.shard_map(
        on_device,
        mesh=torus,
        in_specs=(
            P(WIDE_NARROW, None),
            P(WIDE_NARROW),
            P(WIDE_NARROW),
            P(WIDE_NARROW),
            P(WIDE_NARROW),
            P(WIDE_NARROW),
        ),
        out_specs=(P(WIDE_NARROW, None), P()),
        check_vma=False,
    )
```

profile of v0, /device:TPU:1, one launch (start us, length us, event | category | flops | bytes accessed | tf_op | source)
XLA Modules:
  0.0 323.6 jit_solution(10078858872643697720)
XLA Ops:
  1.5 5.8 %sort.31 = (s32[4096]{0:T(1024)}, s32[4096]{0:T(1024)S(1)}) sort(s32[4096]{0:T(1024)S(1)} %multiply_add_fusion, s32[4096]{0:T(1024)S(1)} %iota.19), dimensions={0}, to_apply=%region_0.0 | sort | flops 49152 | bytes 65536 | tf_op jit(solution)/shard_map/jit(argsort)/sort | solution.py:56
  7.3 23.0 %gather_fusion.2 = s32[4096]{0:T(1024)S(1)} fusion(s32[4096]{0:T(1024)S(1)} %copy-done.1, s32[4096]{0:T(1024)S(1)} %fusion.6), kind=kCustom, calls=%fused_computation.2 | custom fusion | bytes 49152 | tf_op jit(solution)/shard_map/gather | solution.py:64
  30.4 23.0 %gather_fusion.1 = s32[4096]{0:T(1024)S(1)} fusion(s32[4096]{0:T(1024)S(1)} %copy-done.2, s32[4096]{0:T(1024)S(1)} %fusion.6), kind=kCustom, calls=%fused_computation.1 | custom fusion | bytes 49152 | tf_op jit(solution)/shard_map/gather | solution.py:63
  53.4 23.0 %gather_fusion = s32[4096]{0:T(1024)S(1)} fusion(s32[4096]{0:T(1024)S(1)} %copy-done.3, s32[4096]{0:T(1024)S(1)} %fusion.6), kind=kCustom, calls=%fused_computation | custom fusion | bytes 49152 | tf_op jit(solution)/shard_map/gather | solution.py:62
  77.9 15.6 %all-to-all-start = ((s32[256,1,1,3,16]{4,2,3,1,0:T(1,128)}), s32[256,1,1,3,16]{4,2,3,1,0:T(1,128)S(1)}, u32[]{:S(2)}, u32[]{:S(2)}) async-start(s32[256,1,1,3,16]{4,2,3,1,0:T(1,128)} %copy.20), calls=%async_computation | async-start | bytes 786432 | tf_op jit(solution)/shard_map/all_to_all | solution.py:30
  93.6 15.0 %gather_fusion.3 = bf16[4096,128]{1,0:T(8,128)(2,1)} fusion(bf16[4096,128]{1,0:T(8,128)(2,1)S(1)} %copy-done, s32[4096]{0:T(1024)S(1)} %fusion.6), kind=kCustom, calls=%fused_computation.3 | custom fusion | bytes 2113536 | tf_op jit(solution)/shard_map/gather | solution.py:58
  110.7 12.7 %all-to-all-start.1 = ((bf16[256,1,1,16,128]{4,3,2,1,0:T(8,128)(2,1)}), bf16[256,1,1,16,128]{4,3,2,1,0:T(8,128)(2,1)}, u32[]{:S(2)}, u32[]{:S(2)}) async-start(bf16[256,1,1,16,128]{4,3,2,1,0:T(8,128)(2,1)} %bitcast.10), calls=%async_computation.1 | async-start | bytes 2097152 | tf_op jit(solution)/shard_map/all_to_all | solution.py:30
  124.0 28.9 %all-to-all-done.1 = bf16[256,1,1,16,128]{4,3,2,1,0:T(8,128)(2,1)} async-done(((bf16[256,1,1,16,128]{4,3,2,1,0:T(8,128)(2,1)}), bf16[256,1,1,16,128]{4,3,2,1,0:T(8,128)(2,1)}, u32[]{:S(2)}, u32[]{:S(2)}) %all-to-all-start.1) | async-done | bytes 1048608 | tf_op jit(solution)/shard_map/all_to_all | solution.py:30
  154.0 79.1 %while.17 = (s32[]{:T(128)}, bf16[4096,128]{1,0:T(8,128)(2,1)}, f32[]{:T(128)}, s32[4096]{0:T(1024)S(1)}, s32[32,8,1,16]{3,1,0,2:T(8,128)}, /*index=5*/s32[4096]...) while((s32[]{:T(128)}, bf16[4096,128]{1,0:T(8,128)(2,1)}, ...), condition=%wide.wide.region_5.6_spmd.clone, body=%wide.wide.region_1.5_spmd.clone.sunk | while | flops 557979136 | bytes 7565543 | solution.py:97
  154.3 4.1 %fusion.21 = (pred[512]{0:T(512)(128)(4,1)S(1)}, pred[512,4096]{1,0:T(32,128)(4,1)S(1)}) fusion(s32[512]{0:T(512)S(1)} %iota_add_fusion.3, pred[4096]{0:T(1024)(128)(4,1)S(1)} %gt.36, pred[512]{0:T(512)(128)(4,1)S(1)} %dynamic-slice_compare_fusion.3, s32[4096]{0:T(1024)S(1)} %get-tuple-element.400, s32[512]{0:T(512)S(1)} %dynamic_slice.32, ...), kind=kLoop, calls=%fused_computation.9.clone.clone.1 | loop fusion | flops 16776704 | bytes 2141184 | tf_op jit(solution)/shard_map/while/body/eval_jaxpr/reduce_or | solution.py:91
  164.2 4.1 %fusion.21 = (pred[512]{0:T(512)(128)(4,1)S(1)}, pred[512,4096]{1,0:T(32,128)(4,1)S(1)}) fusion(s32[512]{0:T(512)S(1)} %iota_add_fusion.3, pred[4096]{0:T(1024)(128)(4,1)S(1)} %gt.36, pred[512]{0:T(512)(128)(4,1)S(1)} %dynamic-slice_compare_fusion.3, s32[4096]{0:T(1024)S(1)} %get-tuple-element.400, s32[512]{0:T(512)S(1)} %dynamic_slice.32, ...), kind=kLoop, calls=%fused_computation.9.clone.clone.1 | loop fusion | flops 16776704 | bytes 2141184 | tf_op jit(solution)/shard_map/while/body/eval_jaxpr/reduce_or | solution.py:91
  174.1 4.1 %fusion.21 = (pred[512]{0:T(512)(128)(4,1)S(1)}, pred[512,4096]{1,0:T(32,128)(4,1)S(1)}) fusion(s32[512]{0:T(512)S(1)} %iota_add_fusion.3, pred[4096]{0:T(1024)(128)(4,1)S(1)} %gt.36, pred[512]{0:T(512)(128)(4,1)S(1)} %dynamic-slice_compare_fusion.3, s32[4096]{0:T(1024)S(1)} %get-tuple-element.400, s32[512]{0:T(512)S(1)} %dynamic_slice.32, ...), kind=kLoop, calls=%fused_computation.9.clone.clone.1 | loop fusion | flops 16776704 | bytes 2141184 | tf_op jit(solution)/shard_map/while/body/eval_jaxpr/reduce_or | solution.py:91
  184.0 4.1 %fusion.21 = (pred[512]{0:T(512)(128)(4,1)S(1)}, pred[512,4096]{1,0:T(32,128)(4,1)S(1)}) fusion(s32[512]{0:T(512)S(1)} %iota_add_fusion.3, pred[4096]{0:T(1024)(128)(4,1)S(1)} %gt.36, pred[512]{0:T(512)(128)(4,1)S(1)} %dynamic-slice_compare_fusion.3, s32[4096]{0:T(1024)S(1)} %get-tuple-element.400, s32[512]{0:T(512)S(1)} %dynamic_slice.32, ...), kind=kLoop, calls=%fused_computation.9.clone.clone.1 | loop fusion | flops 16776704 | bytes 2141184 | tf_op jit(solution)/shard_map/while/body/eval_jaxpr/reduce_or | solution.py:91
  193.9 4.1 %fusion.21 = (pred[512]{0:T(512)(128)(4,1)S(1)}, pred[512,4096]{1,0:T(32,128)(4,1)S(1)}) fusion(s32[512]{0:T(512)S(1)} %iota_add_fusion.3, pred[4096]{0:T(1024)(128)(4,1)S(1)} %gt.36, pred[512]{0:T(512)(128)(4,1)S(1)} %dynamic-slice_compare_fusion.3, s32[4096]{0:T(1024)S(1)} %get-tuple-element.400, s32[512]{0:T(512)S(1)} %dynamic_slice.32, ...), kind=kLoop, calls=%fused_computation.9.clone.clone.1 | loop fusion | flops 16776704 | bytes 2141184 | tf_op jit(solution)/shard_map/while/body/eval_jaxpr/reduce_or | solution.py:91
  203.8 4.1 %fusion.21 = (pred[512]{0:T(512)(128)(4,1)S(1)}, pred[512,4096]{1,0:T(32,128)(4,1)S(1)}) fusion(s32[512]{0:T(512)S(1)} %iota_add_fusion.3, pred[4096]{0:T(1024)(128)(4,1)S(1)} %gt.36, pred[512]{0:T(512)(128)(4,1)S(1)} %dynamic-slice_compare_fusion.3, s32[4096]{0:T(1024)S(1)} %get-tuple-element.400, s32[512]{0:T(512)S(1)} %dynamic_slice.32, ...), kind=kLoop, calls=%fused_computation.9.clone.clone.1 | loop fusion | flops 16776704 | bytes 2141184 | tf_op jit(solution)/shard_map/while/body/eval_jaxpr/reduce_or | solution.py:91
  213.6 4.1 %fusion.21 = (pred[512]{0:T(512)(128)(4,1)S(1)}, pred[512,4096]{1,0:T(32,128)(4,1)S(1)}) fusion(s32[512]{0:T(512)S(1)} %iota_add_fusion.3, pred[4096]{0:T(1024)(128)(4,1)S(1)} %gt.36, pred[512]{0:T(512)(128)(4,1)S(1)} %dynamic-slice_compare_fusion.3, s32[4096]{0:T(1024)S(1)} %get-tuple-element.400, s32[512]{0:T(512)S(1)} %dynamic_slice.32, ...), kind=kLoop, calls=%fused_computation.9.clone.clone.1 | loop fusion | flops 16776704 | bytes 2141184 | tf_op jit(solution)/shard_map/while/body/eval_jaxpr/reduce_or | solution.py:91
  223.5 4.1 %fusion.21 = (pred[512]{0:T(512)(128)(4,1)S(1)}, pred[512,4096]{1,0:T(32,128)(4,1)S(1)}) fusion(s32[512]{0:T(512)S(1)} %iota_add_fusion.3, pred[4096]{0:T(1024)(128)(4,1)S(1)} %gt.36, pred[512]{0:T(512)(128)(4,1)S(1)} %dynamic-slice_compare_fusion.3, s32[4096]{0:T(1024)S(1)} %get-tuple-element.400, s32[512]{0:T(512)S(1)} %dynamic_slice.32, ...), kind=kLoop, calls=%fused_computation.9.clone.clone.1 | loop fusion | flops 16776704 | bytes 2141184 | tf_op jit(solution)/shard_map/while/body/eval_jaxpr/reduce_or | solution.py:91
  233.0 6.7 %all-to-all-start.2 = ((bf16[256,1,1,16,128]{4,3,2,1,0:T(8,128)(2,1)}), bf16[256,1,1,16,128]{4,3,2,1,0:T(8,128)(2,1)S(1)}, u32[]{:S(2)}, u32[]{:S(2)}) async-start(bf16[256,1,1,16,128]{4,3,2,1,0:T(8,128)(2,1)} %bitcast.66), calls=%async_computation.2 | async-start | bytes 2097152 | tf_op jit(solution)/shard_map/all_to_all | solution.py:30
  239.8 33.2 %psum.28 = f32[]{:T(128)} all-reduce(f32[]{:T(128)} %get-tuple-element.192), channel_id=1, replica_groups=mesh['wide_0'=8,'wide_1'=4,'narrow_0'=4,'narrow_1'=2] {'wide_0'}, use_global_device_ids=true, to_apply=%region_7.8 | all-reduce | flops 1 | bytes 8 | tf_op jit(solution)/shard_map/psum | solution.py:37
  272.9 8.6 %psum.29 = f32[]{:T(128)} all-reduce(f32[]{:T(128)} %psum.28), channel_id=1, replica_groups=mesh['wide_0'=8,'wide_1'=4,'narrow_0'=4,'narrow_1'=2] {'wide_1'}, use_global_device_ids=true, to_apply=%region_8.9 | all-reduce | flops 1 | bytes 8 | tf_op jit(solution)/shard_map/psum | solution.py:37
  281.5 5.8 %sort.32 = (s32[4096]{0:T(1024)}, s32[4096]{0:T(1024)S(1)}) sort(s32[4096]{0:T(1024)S(1)} %get-tuple-element.189, s32[4096]{0:T(1024)S(1)} %iota.21), dimensions={0}, to_apply=%region_6.7 | sort | flops 49152 | bytes 65536 | tf_op jit(solution)/shard_map/jit(argsort)/sort | solution.py:57
  287.3 9.1 %psum.30 = f32[]{:T(128)} all-reduce(f32[]{:T(128)} %psum.29), channel_id=1, replica_groups=mesh['wide_0'=8,'wide_1'=4,'narrow_0'=4,'narrow_1'=2] {'narrow_0'}, use_global_device_ids=true, to_apply=%region_9.10 | all-reduce | flops 1 | bytes 8 | tf_op jit(solution)/shard_map/psum | solution.py:37
  296.5 10.3 %psum.31 = f32[]{:T(128)} all-reduce(f32[]{:T(128)} %psum.30), channel_id=1, replica_groups=mesh['wide_0'=8,'wide_1'=4,'narrow_0'=4,'narrow_1'=2] {'narrow_1'}, use_global_device_ids=true, to_apply=%region_10.11 | all-reduce | flops 1 | bytes 8 | tf_op jit(solution)/shard_map/psum | solution.py:37
  307.5 15.0 %gather_fusion.4 = bf16[4096,128]{1,0:T(8,128)(2,1)} fusion(bf16[4096,128]{1,0:T(8,128)(2,1)S(1)} %bitcast.65, s32[4096]{0:T(1024)S(1)} %fusion.7), kind=kCustom, calls=%fused_computation.4 | custom fusion | bytes 2113536 | tf_op jit(solution)/shard_map/gather | solution.py:102
  (112 shorter events, 46.8 us)
Async XLA Ops:
  0.6 93.0 %copy-start = (bf16[4096,128]{1,0:T(8,128)(2,1)S(1)}, bf16[4096,128]{1,0:T(8,128)(2,1)}, u32[]{:S(2)}) copy-start(bf16[4096,128]{1,0:T(8,128)(2,1)} %param.8) | copy-start | bytes 3145732
  0.6 6.6 %copy-start.1 = (s32[4096]{0:T(1024)S(1)}, s32[4096]{0:T(1024)}, u32[]{:S(2)}) copy-start(s32[4096]{0:T(1024)} %param.11) | copy-start | bytes 49156
  7.3 23.1 %copy-start.2 = (s32[4096]{0:T(1024)S(1)}, s32[4096]{0:T(1024)}, u32[]{:S(2)}) copy-start(s32[4096]{0:T(1024)} %param.10) | copy-start | bytes 49156
  30.3 23.1 %copy-start.3 = (s32[4096]{0:T(1024)S(1)}, s32[4096]{0:T(1024)}, u32[]{:S(2)}) copy-start(s32[4096]{0:T(1024)} %param.9) | copy-start | bytes 49156
  77.9 32.7 %all-to-all-start = ((s32[256,1,1,3,16]{4,2,3,1,0:T(1,128)}), s32[256,1,1,3,16]{4,2,3,1,0:T(1,128)S(1)}, u32[]{:S(2)}, u32[]{:S(2)}) async-start(s32[256,1,1,3,16]{4,2,3,1,0:T(1,128)} %copy.20), calls=%async_computation | async-start | bytes 786432 | tf_op jit(solution)/shard_map/all_to_all | solution.py:30
  110.7 42.2 %all-to-all-start.1 = ((bf16[256,1,1,16,128]{4,3,2,1,0:T(8,128)(2,1)}), bf16[256,1,1,16,128]{4,3,2,1,0:T(8,128)(2,1)}, u32[]{:S(2)}, u32[]{:S(2)}) async-start(bf16[256,1,1,16,128]{4,3,2,1,0:T(8,128)(2,1)} %bitcast.10), calls=%async_computation.1 | async-start | bytes 2097152 | tf_op jit(solution)/shard_map/all_to_all | solution.py:30
  123.4 30.5 %copy-start.4 = (s32[32,8,1,16]{3,1,0,2:T(8,128)}, s32[32,8,1,16]{3,1,0,2:T(8,128)S(1)}, u32[]{:S(2)}) copy-start(s32[32,8,1,16]{3,1,0,2:T(8,128)S(1)} %get-tuple-element.364) | copy-start | bytes 49156
  123.4 30.5 %copy-start.5 = (s32[32,8,1,16]{3,1,0,2:T(8,128)}, s32[32,8,1,16]{3,1,0,2:T(8,128)S(1)}, u32[]{:S(2)}) copy-start(s32[32,8,1,16]{3,1,0,2:T(8,128)S(1)} %get-tuple-element.362) | copy-start | bytes 49156
  233.0 74.4 %all-to-all-start.2 = ((bf16[256,1,1,16,128]{4,3,2,1,0:T(8,128)(2,1)}), bf16[256,1,1,16,128]{4,3,2,1,0:T(8,128)(2,1)S(1)}, u32[]{:S(2)}, u32[]{:S(2)}) async-start(bf16[256,1,1,16,128]{4,3,2,1,0:T(8,128)(2,1)} %bitcast.66), calls=%async_computation.2 | async-start | bytes 2097152 | tf_op jit(solution)/shard_map/all_to_all | solution.py:30
where the time goes:
time: 324 us
  local copies, waits for them, and re-layouts  104 us (32%)
  blocking collectives  61.2 us (19%)
  other arithmetic  59 us (18%)
  starting transfers between devices  35 us (11%)
  waiting for transfers between devices  30.9 us (10%)
  matrix products  25.2 us (8%)
  loops' own time  5.22 us (2%)
    psum x4, blocking collectives, by_axis(): array = lax.psum(array, axis)  61.2 us
    all_to_all x3, starting transfers between devices, joined_exchange(): lax.all_to_all(pieces, axis, split_axis=0, concat_axis=0, tiled=True)  35 us
    reduce_or x8, other arithmetic, full_block(): jnp.any(earlier, axis=1).astype(jnp.float32)  33.1 us
    all_to_all x3, waiting for transfers between devices, joined_exchange(): lax.all_to_all(pieces, axis, split_axis=0, concat_axis=0, tiled=True)  30.9 us
    dot_general x8, matrix products, full_block(): jnp.dot(same.astype(jnp.bfloat16), flat_rows, preferred_element_type=jnp....  25.2 us
    gather x1, local copies, waits for them, and re-layouts, on_device(): live[sort_order].reshape(shaped)  23 us
    gather x1, local copies, waits for them, and re-layouts, on_device(): second_key[sort_order].reshape(shaped)  23 us
    gather x1, local copies, waits for them, and re-layouts, on_device(): first_key[sort_order].reshape(shaped)  23 us
  transfers between devices with their start and end apart: 3, of which 2 were waited for; matrix products, arithmetic and copies ran while one was open for 7% of the time, Pallas kernels for 0%

commit v1 on v0

v1 whole, which is shorter than its diff:
```python
import functools

import jax
import jax.numpy as jnp
from jax import lax
from jax.experimental import pallas as pl
from jax.experimental.pallas import tpu as pltpu
from jax.sharding import Mesh
from jax.sharding import PartitionSpec as P

AXES = ("z", "x", "y", "c")
MESH_ID = pl.DeviceIdType.MESH
f32, bf16, i32 = jnp.float32, jnp.bfloat16, jnp.int32
SLOT = 16
LANES = 128


def onehot(mask):
    return jnp.where(mask, 1.0, 0.0).astype(bf16)


def rows_at(start, size, align):
    return pl.ds(pl.multiple_of(start, align), size)


class Plan:
    def __init__(self, dims, chunk, block):
        self.dims = dims
        self.devices = 1
        for n in dims:
            self.devices *= n
        self.mul = 37 % self.devices
        self.mul_inverse = pow(self.mul, -1, self.devices)
        self.rows = self.devices * SLOT
        self.chunk = chunk
        self.chunks = self.rows // chunk
        self.chunk_slots = chunk // SLOT
        self.block = block
        self.row_lines = self.rows // LANES

    def partner(self, slot, sign):
        offset = lax.rem(slot * self.mul, self.devices)
        ids = []
        for n, axis in reversed(list(zip(self.dims, AXES))):
            step = lax.rem(offset, n)
            offset = offset // n
            ids.append(lax.rem(lax.axis_index(axis) + (step if sign > 0 else n - step), n))
        return tuple(reversed(ids))

    def slot_of(self, coords):
        offset = jnp.zeros_like(coords[0])
        for n, axis, at in zip(self.dims, AXES, coords):
            offset = offset * n + lax.rem(at - lax.axis_index(axis) + n, n)
        return lax.rem(offset * self.mul_inverse, self.devices)


def column_form(lines, col_ref, plan):
    turned = jnp.transpose(lines)
    for b in range(plan.row_lines):
        col_ref[pl.ds(b * LANES, LANES), :] = jnp.broadcast_to(turned[:, b : b + 1], (LANES, LANES))


def wide_line(ref, chunk_index, plan):
    n = plan.chunk // LANES
    return jnp.concatenate([ref[pl.ds(chunk_index * n + t, 1), :] for t in range(n)], axis=1)


def kernel(plan, pay_hbm, ord_ref, k1_ref, k2_ref, out_hbm, dup_ref, pay, send, recv, mean, ret, col_a, col_b,
           tag_send, tag_recv, line_a, line_b, acc, back, io_sem, tag_sems, pay_send_sem, pay_sems, ret_send_sem, ret_sems):
    dev, rows, chunk, block = plan.devices, plan.rows, plan.chunk, plan.block
    load = pltpu.make_async_copy(pay_hbm, pay, io_sem)
    load.start()
    barrier = pltpu.get_barrier_semaphore()

    def greet(slot, carry):
        pl.semaphore_signal(barrier, inc=1, device_id=plan.partner(slot, 1), device_id_type=MESH_ID)
        return carry

    lax.fori_loop(1, dev, greet, 0)

    part = lax.broadcasted_iota(i32, (8, LANES), 1) // SLOT
    sub = lax.broadcasted_iota(i32, (8, LANES), 0)
    mine = part == sub
    half = part == lax.rem(sub + 4, 8)
    for a in range(plan.row_lines):
        one = jnp.broadcast_to(k1_ref[pl.ds(a, 1), :], (8, LANES))
        two = jnp.broadcast_to(pltpu.roll(k2_ref[pl.ds(a, 1), :], LANES // 2, 1), (8, LANES))
        tag_send[pl.ds(8 * a, 8), :] = jnp.where(mine, one, two)
    column_form(ord_ref[...], col_a, plan)
    load.wait()

    deep = min(1024, rows)
    lane = lax.broadcasted_iota(i32, (chunk, deep), 1)

    def permute(c, carry):
        at = rows_at(c * chunk, chunk, chunk)
        want = jnp.concatenate([col_a[at, :]] * (deep // LANES), axis=1)
        total = jnp.zeros((chunk, LANES), f32)
        for k in range(rows // deep):
            pick = onehot(want - k * deep == lane)
            total = total + jnp.dot(pick, pay[pl.ds(k * deep, deep), :], preferred_element_type=f32)
        send[at, :] = total.astype(bf16)
        return carry

    lax.fori_loop(0, plan.chunks, permute, 0)
    pl.semaphore_wait(barrier, dev - 1)

    def send_tag(slot, carry):
        at = pl.ds(slot, 1)
        pltpu.make_async_remote_copy(
            src_ref=tag_send.at[at], dst_ref=tag_recv.at[at], send_sem=tag_sems.at[0], recv_sem=tag_sems.at[1],
            device_id=plan.partner(slot, 1), device_id_type=MESH_ID,
        ).start()
        return carry

    lax.fori_loop(1, dev, send_tag, 0)

    def send_row(slot, carry):
        at = rows_at(slot * SLOT, SLOT, SLOT)
        pltpu.make_async_remote_copy(
            src_ref=send.at[at], dst_ref=recv.at[at], send_sem=pay_send_sem,
            recv_sem=pay_sems.at[slot // plan.chunk_slots],
            device_id=plan.partner(slot, 1), device_id_type=MESH_ID,
        ).start()
        return carry

    lax.fori_loop(1, dev, send_row, 0)
    recv[pl.ds(0, SLOT), :] = send[pl.ds(0, SLOT), :]
    tag_recv[pl.ds(0, 1), :] = tag_send[pl.ds(0, 1), :]
    acc[...] = jnp.zeros_like(acc)
    back[...] = jnp.zeros_like(back)

    others = pl.ds(1, dev - 1)
    pltpu.make_async_copy(tag_send.at[others], tag_recv.at[others], tag_sems.at[1]).wait()
    for a in range(plan.row_lines):
        got = tag_recv[pl.ds(8 * a, 8), :]
        line_a[pl.ds(a, 1), :] = jnp.sum(jnp.where(mine, got, 0), axis=0, keepdims=True)
        line_b[pl.ds(a, 1), :] = pltpu.roll(jnp.sum(jnp.where(half, got, 0), axis=0, keepdims=True), LANES // 2, 1)
    column_form(line_a[...], col_a, plan)
    column_form(line_b[...], col_b, plan)
    keys = line_a[...]
    line_a[...] = jnp.where(keys < 0, -2, keys)

    def wait_chunk(c, src, dst, sem, first):
        at = rows_at(c * chunk, chunk, chunk) if not first else pl.ds(SLOT, chunk - SLOT)
        pltpu.make_async_copy(src.at[at], dst.at[at], sem).wait()

    def add_pairs(c):
        rhs = jnp.concatenate([recv[rows_at(c * chunk, chunk, chunk), :], jnp.ones((chunk, LANES), bf16)], axis=1)
        one, two = wide_line(line_a, c, plan), wide_line(line_b, c, plan)
        for b in range(rows // block):
            at = pl.ds(b * block, block)
            col_one = jnp.concatenate([col_a[at, :]] * (chunk // LANES), axis=1)
            col_two = jnp.concatenate([col_b[at, :]] * (chunk // LANES), axis=1)
            same = onehot((col_one == one) & (col_two == two))
            acc[at, :] += jnp.dot(same, rhs, preferred_element_type=f32)

    wait_chunk(0, send, recv, pay_sems.at[0], True)
    add_pairs(0)

    def pairs(c, carry):
        wait_chunk(c, send, recv, pay_sems.at[c], False)
        add_pairs(c)
        return carry

    lax.fori_loop(1, plan.chunks, pairs, 0)

    piece = min(256, rows)
    slots = piece // SLOT

    def send_back(slot, carry):
        at = rows_at(slot * SLOT, SLOT, SLOT)
        pltpu.make_async_remote_copy(
            src_ref=mean.at[at], dst_ref=ret.at[at], send_sem=ret_send_sem,
            recv_sem=ret_sems.at[slot // plan.chunk_slots],
            device_id=plan.partner(slot, -1), device_id_type=MESH_ID,
        ).start()
        return carry

    def finish(p, dups):
        at = rows_at(p * piece, piece, piece)
        count = acc[at, pl.ds(LANES, LANES)]
        inverse = 1.0 / jnp.maximum(count, 1.0)
        mean[at, :] = (acc[at, pl.ds(0, LANES)] * inverse).astype(bf16)
        again = jnp.where(count > 0.0, 1.0 - inverse, 0.0)
        return dups + jnp.sum(again.reshape(piece // 8, 8, LANES), axis=0)

    def finish_and_send(p, dups):
        dups = finish(p, dups)
        first = (p - 1) * slots
        lax.fori_loop(jnp.maximum(first, 1), first + slots, send_back, 0)
        return dups

    dups = finish(0, jnp.zeros((8, LANES), f32))
    dups = lax.fori_loop(1, rows // piece, finish_and_send, dups)
    dup_ref[...] = dups
    ret[pl.ds(0, SLOT), :] = mean[pl.ds(0, SLOT), :]
    lax.fori_loop(max(dev - slots, 1), dev, send_back, 0)

    def add_back(c, last):
        rhs = ret[rows_at(c * chunk, chunk, chunk), :]
        order = wide_line(ord_ref, c, plan)
        own = lax.broadcasted_iota(i32, (block, chunk), 0)
        for b in range(rows // block):
            at = pl.ds(b * block, block)
            pick = onehot(own == order - b * block)
            total = back[at, :] + jnp.dot(pick, rhs, preferred_element_type=f32)
            if last:
                pay[at, :] = total.astype(bf16)
            else:
                back[at, :] = total

    wait_chunk(0, mean, ret, ret_sems.at[0], True)
    add_back(0, False)

    def backs(c, carry):
        wait_chunk(c, mean, ret, ret_sems.at[c], False)
        add_back(c, False)
        return carry

    lax.fori_loop(1, plan.chunks - 1, backs, 0)
    wait_chunk(plan.chunks - 1, mean, ret, ret_sems.at[plan.chunks - 1], False)
    add_back(plan.chunks - 1, True)
    store = pltpu.make_async_copy(pay, out_hbm, io_sem)
    store.start()
    sent = pl.ds(SLOT, rows - SLOT)
    pltpu.make_async_copy(tag_send.at[others], tag_recv.at[others], tag_sems.at[0]).wait()
    pltpu.make_async_copy(send.at[sent], recv.at[sent], pay_send_sem).wait()
    pltpu.make_async_copy(mean.at[sent], ret.at[sent], ret_send_sem).wait()
    store.wait()


def exchange(plan, payload, order, key_one, key_two):
    rows, dev, lines = plan.rows, plan.devices, plan.row_lines
    vmem, hbm = pl.BlockSpec(memory_space=pltpu.VMEM), pl.BlockSpec(memory_space=pl.ANY)
    tile = lambda n, m, t: pltpu.VMEM((n, m), t)
    return pl.pallas_call(
        functools.partial(kernel, plan),
        out_shape=(jax.ShapeDtypeStruct((rows, LANES), bf16), jax.ShapeDtypeStruct((8, LANES), f32)),
        in_specs=[hbm, vmem, vmem, vmem],
        out_specs=(hbm, vmem),
        scratch_shapes=[
            *[tile(rows, LANES, bf16) for _ in range(5)],
            tile(rows, LANES, i32),
            tile(rows, LANES, i32),
            tile(dev, LANES, i32),
            tile(dev, LANES, i32),
            tile(lines, LANES, i32),
            tile(lines, LANES, i32),
            tile(rows, 2 * LANES, f32),
            tile(rows, LANES, f32),
            pltpu.SemaphoreType.DMA,
            pltpu.SemaphoreType.DMA((2,)),
            pltpu.SemaphoreType.DMA,
            pltpu.SemaphoreType.DMA((plan.chunks,)),
            pltpu.SemaphoreType.DMA,
            pltpu.SemaphoreType.DMA((plan.chunks,)),
        ],
        compiler_params=pltpu.CompilerParams(
            collective_id=0, has_side_effects=True, vmem_limit_bytes=48 * 2**20
        ),
        name="filter",
    )(payload, order, key_one, key_two)


def on_device(plan, payload, first_key, second_key, live, first_bucket, second_bucket):
    nz, nx, ny, nc = plan.dims
    coords = (first_bucket // nx, lax.rem(first_bucket, nx), second_bucket // nc, lax.rem(second_bucket, nc))
    place = plan.slot_of(coords) * plan.rows + lax.iota(i32, plan.rows)
    key_one = jnp.where(live > 0, first_key, -1)
    place, key_one, key_two = lax.sort((place, key_one, second_key), num_keys=1, is_stable=False)
    lines = (plan.row_lines, LANES)
    group_mean, dups = exchange(
        plan, payload, lax.rem(place, plan.rows).reshape(lines), key_one.reshape(lines), key_two.reshape(lines)
    )
    own = jnp.round(jnp.sum(dups[:, 0]))
    return group_mean, lax.psum(own, AXES).astype(i32)


def build(torus, plan):
    rows = P(AXES)
    return jax.shard_map(
        functools.partial(on_device, plan),
        mesh=torus,
        in_specs=(P(AXES, None), rows, rows, rows, rows, rows),
        out_specs=(P(AXES, None), P()),
        check_vma=False,
    )


def solution(mesh):
    dims = (8, 4, 4, 2)
    return build(Mesh(mesh.devices.reshape(dims), AXES), Plan(dims, 512, 1024))
```

time: 324 us -> 188 us (0.58)
  local copies, waits for them, and re-layouts: 104 us -> 2.9 us
  Pallas kernels: 0 us -> 101 us
  other arithmetic: 59 us -> 6.41 us
  starting transfers between devices: 35 us -> 0 us
  waiting for transfers between devices: 30.9 us -> 0 us
  matrix products: 25.2 us -> 0 us
  blocking collectives: 61.2 us -> 74.4 us
  loops' own time: 5.22 us -> 0 us
    pallas_call x0 -> x1, Pallas kernels: none -> 101 us  [exchange(): pl.pallas_call(functools.partial(kernel, plan), out_shape=(jax.ShapeDtype...]
    gather x5 -> x0, local copies, waits for them, and re-layouts: 99.2 us -> none  [the longest x1 23 us: on_device(): live[sort_order].reshape(shaped)]
    all_to_all x3 -> x0, starting transfers between devices: 35 us -> none  [joined_exchange(): lax.all_to_all(pieces, axis, split_axis=0, concat_axis=0, tiled=True)]
    reduce_or x8 -> x0, other arithmetic: 33.1 us -> none  [full_block(): jnp.any(earlier, axis=1).astype(jnp.float32)]
    all_to_all x3 -> x0, waiting for transfers between devices: 30.9 us -> none  [joined_exchange(): lax.all_to_all(pieces, axis, split_axis=0, concat_axis=0, tiled=True)]
    dot_general x8 -> x0, matrix products: 25.2 us -> none  [full_block(): jnp.dot(same.astype(jnp.bfloat16), flat_rows, preferred_element_type=jnp....]
    psum x4 -> x1, blocking collectives: 61.2 us -> 74.4 us  [on_device(): return (group_mean, lax.psum(own, AXES).astype(i32))]
    reduce_sum x16 -> x1, other arithmetic: 12.6 us -> 0.6 us  [on_device(): own = jnp.round(jnp.sum(dups[:, 0]))]
  transfers between devices with their start and end apart: 3 -> 0, of which waited for: 2 -> 0; matrix products, arithmetic and copies ran while one was open for 7% -> 0% of each run, Pallas kernels for 0% -> 0%
where the time goes in v1:
time: 188 us
  Pallas kernels  101 us (54%)
  blocking collectives  74.4 us (40%)
  other arithmetic  6.41 us (3%)
  between operations  3.12 us (2%)
  local copies, waits for them, and re-layouts  2.9 us (2%)
    pallas_call x1, Pallas kernels, exchange(): pl.pallas_call(functools.partial(kernel, plan), out_shape=(jax.ShapeDtype...  101 us
    psum x1, blocking collectives, on_device(): return (group_mean, lax.psum(own, AXES).astype(i32))  74.4 us
    sort x1, other arithmetic, on_device(): lax.sort((place, key_one, second_key), num_keys=1, is_stable=False)  4.98 us

profile of v1, /device:TPU:1, one launch (start us, length us, event | category | flops | bytes accessed | tf_op | source)
XLA Modules:
  0.0 187.6 jit_solution(10356562305944308677)
XLA Ops:
  0.6 0.0 copy-start.1
  0.6 0.7 copy-done.1
  1.4 0.0 copy-start.2
  1.4 0.8 fusion.16
  2.2 0.0 copy-done.2
  2.2 5.0 %sort.21 = (s32[4096]{0:T(1024)S(1)}, s32[4096]{0:T(1024)S(1)}, s32[4096]{0:T(1024)S(1)}) sort(s32[4096]{0:T(1024)S(1)} %get-tuple-element.12, s32[4096]{0:T(1024)S(1)} %get-tuple-element.13, s32[4096]{0:T(1024)S(1)} %copy-done.2), dimensions={0}, to_apply=%region_0.1 | sort | flops 49152 | bytes 98304 | tf_op jit(solution)/shard_map/sort | solution.py:271
  7.2 0.0 copy-start
  7.2 1.2 copy-done
  8.4 100.8 %filter.1 = (bf16[4096,128]{1,0:T(8,128)(2,1)S(1)}, f32[8,128]{1,0:T(8,128)S(1)}) custom-call(bf16[4096,128]{1,0:T(8,128)(2,1)S(1)} %copy-done, s32[32,128]{1,0:T(8,128)S(1)} %fusion.18.ord_ref, s32[32,128]{1,0:T(8,128)S(1)} %bitcast.4, s32[32,128]{1,0:T(8,128)S(1)} %bitcast.5), custom_call_target="tpu_custom_call" | custom-call | tf_op jit(solution)/shard_map/filter/pallas_call | solution.py:237
  109.2 0.6 slice_reduce_fusion
  110.4 74.4 %psum.7 = f32[]{:T(128)} all-reduce(f32[]{:T(128)S(6)} %round.4), channel_id=1, replica_groups=mesh['z'=8,'x'=4,'y'=4,'c'=2] {'z','x','y','c'}, use_global_device_ids=true, to_apply=%region_2.3 | all-reduce | flops 1 | bytes 8 | tf_op jit(solution)/shard_map/psum | solution.py:277
  185.5 1.0 copy.9
  (1 shorter events, 0.0 us)
Async XLA Ops:
  0.6 0.7 copy-start.1
  1.4 0.8 copy-start.2
  7.2 1.2 copy-start

commit v2 on v1

v2 whole, which is shorter than its diff:
```python
import functools

import jax
import jax.numpy as jnp
from jax import lax
from jax.experimental import pallas as pl
from jax.experimental.pallas import tpu as pltpu
from jax.sharding import Mesh
from jax.sharding import PartitionSpec as P

AXES = ("z", "x", "y", "c")
MESH_ID = pl.DeviceIdType.MESH
f32, bf16, i32 = jnp.float32, jnp.bfloat16, jnp.int32
SLOT = 16
LANES = 128


def onehot(mask):
    return jnp.where(mask, 1.0, 0.0).astype(bf16)


def rows_at(start, size, align):
    return pl.ds(pl.multiple_of(start, align), size)


class Plan:
    def __init__(self, dims, chunk, block, early, unrolled=False):
        self.dims = dims
        self.plane = dims[1] * dims[2] * dims[3]
        self.devices = dims[0] * self.plane
        self.units = dims[0]
        self.rows = self.devices * SLOT
        self.chunk = chunk
        self.chunks = self.rows // chunk
        self.chunk_slots = chunk // SLOT
        self.block = block
        self.early = early
        self.row_lines = self.rows // LANES
        self.unrolled = unrolled
        self.first = (dims[1] // 2, dims[2] // 2, dims[3] // 2)
        at = [(n - f) % n for n, f in zip(dims[1:], self.first)]
        self.own_rest = (at[0] * dims[2] + at[1]) * dims[3] + at[2]
        self.own_slot = self.devices - self.plane + self.own_rest

    def loop(self, low, high, body):
        if self.unrolled:
            for i in range(low, high):
                body(i)
        else:
            lax.fori_loop(low, high, lambda i, carry: (body(i), carry)[1], 0)

    def slot_of(self, coords):
        nz = self.dims[0]
        steps = [lax.rem(at - lax.axis_index(axis) + n, n) for n, axis, at in zip(self.dims, AXES, coords)]
        rest = jnp.zeros_like(steps[0])
        for n, f, step in zip(self.dims[1:], self.first, steps[1:]):
            rest = rest * n + lax.rem(step - f + n, n)
        far = jnp.minimum(steps[0], nz - steps[0])
        pair = self.plane + (nz // 2 - 1 - far) * 2 * self.plane + 2 * rest + (steps[0] > nz // 2).astype(i32)
        slot = jnp.where(far == nz // 2, rest, pair)
        return jnp.where(far == 0, self.devices - self.plane + rest, slot)


class Partners:
    def __init__(self, plan, sign):
        self.plan, self.sign = plan, sign
        self.me = [lax.axis_index(axis) for axis in AXES]
        nx, ny, nc = plan.dims[1:]
        self.tails = [
            (self.shift(2, ty + plan.first[1]), self.shift(3, tc + plan.first[2])) for ty in range(ny) for tc in range(nc)
        ]

    def shift(self, dim, step):
        n = self.plan.dims[dim]
        return lax.rem(self.me[dim] + (step if self.sign > 0 else 2 * n - step), n)

    def unit(self, u, act):
        plan = self.plan
        nz, nx = plan.dims[:2]
        width = len(self.tails)
        base = u * plan.plane
        if isinstance(u, int) and u == 0:
            ups = [(self.shift(0, nz // 2), 0)]
            low, high, origin, stride = 0, nx, 0, 1
        elif isinstance(u, int) and u == plan.units - 1:
            for tx in range(nx):
                for k, tail in enumerate(self.tails):
                    rest = tx * width + k
                    if rest != plan.own_rest:
                        act(base + rest, (self.me[0], self.shift(1, tx + plan.first[0]), *tail))
            return
        else:
            far = nz // 2 - 1 - (u - 1) // 2
            ups = [(self.shift(0, far), 0), (self.shift(0, nz - far), 1)]
            low, high, origin, stride = 0, nx // 2, lax.rem(u - 1, 2) * (nx // 2), 2

        def line(t, carry):
            x = self.shift(1, origin + t + plan.first[0])
            for k, tail in enumerate(self.tails):
                for z, plus in ups:
                    act(base + stride * (t * width + k) + plus, (z, x, *tail))
            return carry

        lax.fori_loop(low, high, line, 0)

    def all(self, act):
        self.unit(0, act)
        self.plan.loop(1, self.plan.units - 1, lambda u: self.unit(u, act))
        self.unit(self.plan.units - 1, act)


def column_form(lines, col_ref, plan):
    turned = jnp.transpose(lines)
    for b in range(plan.row_lines):
        col_ref[pl.ds(b * LANES, LANES), :] = jnp.broadcast_to(turned[:, b : b + 1], (LANES, LANES))


def wide_line(ref, chunk_index, plan):
    n = plan.chunk // LANES
    return jnp.concatenate([ref[pl.ds(chunk_index * n + t, 1), :] for t in range(n)], axis=1)


def kernel(plan, pay_hbm, ord_ref, k1_ref, k2_ref, out_ref, dup_ref, pay, send, recv, mean, ret, col_a, col_b,
           tag_send, tag_recv, line_a, line_b, acc, back, near, far, io_sem, tag_sems, pay_send_sem, pay_sems,
           ret_send_sem, ret_sems, dup_sems):
    dev, rows, chunk, block, plane = plan.devices, plan.rows, plan.chunk, plan.block, plan.plane
    to, source = Partners(plan, 1), Partners(plan, -1)
    load = pltpu.make_async_copy(pay_hbm, pay, io_sem)
    load.start()
    barrier = pltpu.get_barrier_semaphore()
    to.all(lambda slot, who: pl.semaphore_signal(barrier, inc=1, device_id=who, device_id_type=MESH_ID))

    part = lax.broadcasted_iota(i32, (8, LANES), 1) // SLOT
    sub = lax.broadcasted_iota(i32, (8, LANES), 0)
    mine = part == sub
    half = part == lax.rem(sub + 4, 8)
    for a in range(plan.row_lines):
        one = jnp.broadcast_to(k1_ref[pl.ds(a, 1), :], (8, LANES))
        two = jnp.broadcast_to(pltpu.roll(k2_ref[pl.ds(a, 1), :], LANES // 2, 1), (8, LANES))
        tag_send[pl.ds(8 * a, 8), :] = jnp.where(mine, one, two)
    column_form(ord_ref[...], col_a, plan)
    load.wait()

    deep = min(1024, rows)
    lane = lax.broadcasted_iota(i32, (chunk, deep), 1)

    def permute(c):
        at = rows_at(c * chunk, chunk, chunk)
        want = jnp.concatenate([col_a[at, :]] * (deep // LANES), axis=1)
        total = jnp.zeros((chunk, LANES), f32)
        for k in range(rows // deep):
            pick = onehot(want - k * deep == lane)
            total = total + jnp.dot(pick, pay[pl.ds(k * deep, deep), :], preferred_element_type=f32)
        send[at, :] = total.astype(bf16)

    def send_tag(slot, who):
        at = pl.ds(slot, 1)
        pltpu.make_async_remote_copy(
            src_ref=tag_send.at[at], dst_ref=tag_recv.at[at], send_sem=tag_sems.at[0], recv_sem=tag_sems.at[1],
            device_id=who, device_id_type=MESH_ID,
        ).start()

    def send_row(slot, who):
        at = rows_at(slot * SLOT, SLOT, SLOT)
        pltpu.make_async_remote_copy(
            src_ref=send.at[at], dst_ref=recv.at[at], send_sem=pay_send_sem,
            recv_sem=pay_sems.at[slot // plan.chunk_slots], device_id=who, device_id_type=MESH_ID,
        ).start()

    def send_chunk(group, c, act):
        per = plan.units // plan.chunks
        for i in range(per):
            group.unit(c * per + i, act)

    early = plan.early
    plan.loop(0, early, permute)
    pl.semaphore_wait(barrier, dev - 1)
    to.all(send_tag)
    send_chunk(to, 0, send_row)
    plan.loop(1, early - 1, lambda c: send_chunk(to, c, send_row))

    def permute_and_send(c):
        permute(c)
        send_chunk(to, c - 1, send_row)

    plan.loop(early, plan.chunks, permute_and_send)
    own = rows_at(plan.own_slot * SLOT, SLOT, SLOT)
    own_line = pl.ds(plan.own_slot, 1)
    recv[own, :] = send[own, :]
    tag_recv[own_line, :] = tag_send[own_line, :]
    acc[...] = jnp.zeros_like(acc)
    back[...] = jnp.zeros_like(back)
    send_chunk(to, plan.chunks - 1, send_row)

    others = pl.ds(0, dev - 1)
    pltpu.make_async_copy(tag_send.at[others], tag_recv.at[others], tag_sems.at[1]).wait()
    for a in range(plan.row_lines):
        got = tag_recv[pl.ds(8 * a, 8), :]
        line_a[pl.ds(a, 1), :] = jnp.sum(jnp.where(mine, got, 0), axis=0, keepdims=True)
        line_b[pl.ds(a, 1), :] = pltpu.roll(jnp.sum(jnp.where(half, got, 0), axis=0, keepdims=True), LANES // 2, 1)
    column_form(line_a[...], col_a, plan)
    column_form(line_b[...], col_b, plan)
    keys = line_a[...]
    line_a[...] = jnp.where(keys < 0, -2, keys)

    def wait_chunk(src, dst, sems, c, last=False):
        at = pl.ds(0, chunk - SLOT if last else chunk)
        pltpu.make_async_copy(src.at[at], dst.at[at], sems.at[c]).wait()

    def add_pairs(c):
        rhs = jnp.concatenate([recv[rows_at(c * chunk, chunk, chunk), :], jnp.ones((chunk, LANES), bf16)], axis=1)
        one, two = wide_line(line_a, c, plan), wide_line(line_b, c, plan)
        for b in range(rows // block):
            at = pl.ds(b * block, block)
            col_one = jnp.concatenate([col_a[at, :]] * (chunk // LANES), axis=1)
            col_two = jnp.concatenate([col_b[at, :]] * (chunk // LANES), axis=1)
            same = onehot((col_one == one) & (col_two == two))
            acc[at, :] += jnp.dot(same, rhs, preferred_element_type=f32)

    final = plan.chunks - 1

    def pairs(c):
        wait_chunk(send, recv, pay_sems, c)
        add_pairs(c)

    plan.loop(0, final, pairs)
    wait_chunk(send, recv, pay_sems, final, True)
    add_pairs(final)

    piece = min(256, chunk)

    def counts(p, dups):
        at = rows_at(p * piece, piece, piece)
        count = acc[at, pl.ds(LANES, LANES)]
        inverse = 1.0 / jnp.maximum(count, 1.0)
        acc[at, pl.ds(LANES, LANES)] = inverse
        again = jnp.where(count > 0.0, 1.0 - inverse, 0.0)
        return dups + jnp.sum(again.reshape(piece // 8, 8, LANES), axis=0)

    dups = lax.fori_loop(0, rows // piece, counts, jnp.zeros((8, LANES), f32))
    near[pl.ds(plan.own_rest, 1), :] = jnp.floor(jnp.sum(dups, axis=0, keepdims=True) + 0.5)

    def finish(p):
        at = rows_at(p * piece, piece, piece)
        mean[at, :] = (acc[at, pl.ds(0, LANES)] * acc[at, pl.ds(LANES, LANES)]).astype(bf16)

    def send_near(slot, who):
        rest = slot - (dev - plane)
        pltpu.make_async_remote_copy(
            src_ref=near.at[pl.ds(plan.own_rest, 1)], dst_ref=near.at[pl.ds(rest, 1)], send_sem=dup_sems.at[0],
            recv_sem=dup_sems.at[1], device_id=who, device_id_type=MESH_ID,
        ).start()

    def send_back(slot, who):
        at = rows_at(slot * SLOT, SLOT, SLOT)
        pltpu.make_async_remote_copy(
            src_ref=mean.at[at], dst_ref=ret.at[at], send_sem=ret_send_sem,
            recv_sem=ret_sems.at[slot // plan.chunk_slots], device_id=who, device_id_type=MESH_ID,
        ).start()

    pieces = chunk // piece

    def finish_chunk(c):
        for i in range(pieces):
            finish(c * pieces + i)

    def finish_and_send(c):
        finish_chunk(c)
        send_chunk(source, c - 1, send_back)

    finish_chunk(0)
    finish_chunk(1)
    to.unit(plan.units - 1, send_near)
    send_chunk(source, 0, send_back)
    plan.loop(2, plan.chunks, finish_and_send)
    ret[own, :] = mean[own, :]

    near_rows = pl.ds(0, plane - 1)
    pltpu.make_async_copy(near.at[near_rows], near.at[near_rows], dup_sems.at[1]).wait()
    far[pl.ds(0, 1), :] = jnp.sum(near[...], axis=0, keepdims=True)
    send_chunk(source, plan.chunks - 1, send_back)
    nz = plan.dims[0]
    for step in range(1, nz):
        pltpu.make_async_remote_copy(
            src_ref=far.at[pl.ds(0, 1)], dst_ref=far.at[pl.ds(step, 1)], send_sem=dup_sems.at[2],
            recv_sem=dup_sems.at[3], device_id=(to.shift(0, step), *to.me[1:]), device_id_type=MESH_ID,
        ).start()

    def add_back(c, last):
        rhs = ret[rows_at(c * chunk, chunk, chunk), :]
        order = wide_line(ord_ref, c, plan)
        own_row = lax.broadcasted_iota(i32, (block, chunk), 0)
        for b in range(rows // block):
            at = pl.ds(b * block, block)
            pick = onehot(own_row == order - b * block)
            total = back[at, :] + jnp.dot(pick, rhs, preferred_element_type=f32)
            if last:
                out_ref[at, :] = total.astype(bf16)
            else:
                back[at, :] = total

    def backs(c):
        wait_chunk(mean, ret, ret_sems, c)
        add_back(c, False)

    plan.loop(0, final, backs)
    far_rows = pl.ds(0, nz - 1)
    pltpu.make_async_copy(far.at[far_rows], far.at[far_rows], dup_sems.at[3]).wait()
    dup_ref[...] = jnp.broadcast_to(jnp.sum(far[...], axis=0, keepdims=True), (8, LANES))
    wait_chunk(mean, ret, ret_sems, final, True)
    add_back(final, True)
    sent = pl.ds(0, rows - SLOT)
    pltpu.make_async_copy(tag_send.at[others], tag_recv.at[others], tag_sems.at[0]).wait()
    pltpu.make_async_copy(send.at[sent], recv.at[sent], pay_send_sem).wait()
    pltpu.make_async_copy(mean.at[sent], ret.at[sent], ret_send_sem).wait()
    pltpu.make_async_copy(near.at[near_rows], near.at[near_rows], dup_sems.at[0]).wait()
    pltpu.make_async_copy(far.at[far_rows], far.at[far_rows], dup_sems.at[2]).wait()


def exchange(plan, payload, order, key_one, key_two):
    rows, dev, lines = plan.rows, plan.devices, plan.row_lines
    vmem, hbm = pl.BlockSpec(memory_space=pltpu.VMEM), pl.BlockSpec(memory_space=pltpu.HBM)
    tile = lambda n, m, t: pltpu.VMEM((n, m), t)
    return pl.pallas_call(
        functools.partial(kernel, plan),
        out_shape=(jax.ShapeDtypeStruct((rows, LANES), bf16), jax.ShapeDtypeStruct((8, LANES), f32)),
        in_specs=[hbm, vmem, vmem, vmem],
        out_specs=(vmem, vmem),
        scratch_shapes=[
            *[tile(rows, LANES, bf16) for _ in range(5)],
            tile(rows, LANES, i32),
            tile(rows, LANES, i32),
            tile(dev, LANES, i32),
            tile(dev, LANES, i32),
            tile(lines, LANES, i32),
            tile(lines, LANES, i32),
            tile(rows, 2 * LANES, f32),
            tile(rows, LANES, f32),
            tile(plan.plane, LANES, f32),
            tile(plan.dims[0], LANES, f32),
            pltpu.SemaphoreType.DMA,
            pltpu.SemaphoreType.DMA((2,)),
            pltpu.SemaphoreType.DMA,
            pltpu.SemaphoreType.DMA((plan.chunks,)),
            pltpu.SemaphoreType.DMA,
            pltpu.SemaphoreType.DMA((plan.chunks,)),
            pltpu.SemaphoreType.DMA((4,)),
        ],
        compiler_params=pltpu.CompilerParams(
            collective_id=0, has_side_effects=True, vmem_limit_bytes=48 * 2**20
        ),
        name="filter",
    )(payload, order, key_one, key_two)


def on_device(plan, payload, first_key, second_key, live, first_bucket, second_bucket):
    nz, nx, ny, nc = plan.dims
    coords = (first_bucket // nx, lax.rem(first_bucket, nx), second_bucket // nc, lax.rem(second_bucket, nc))
    place = plan.slot_of(coords) * plan.rows + lax.iota(i32, plan.rows)
    key_one = jnp.where(live > 0, first_key, -1)
    place, key_one, key_two = lax.sort((place, key_one, second_key), num_keys=1, is_stable=False)
    lines = (plan.row_lines, LANES)
    group_mean, dups = exchange(
        plan, payload, lax.rem(place, plan.rows).reshape(lines), key_one.reshape(lines), key_two.reshape(lines)
    )
    return group_mean, dups[0, 0].astype(i32)


def build(torus, plan):
    rows = P(AXES)
    return jax.shard_map(
        functools.partial(on_device, plan),
        mesh=torus,
        in_specs=(P(AXES, None), rows, rows, rows, rows, rows),
        out_specs=(P(AXES, None), P()),
        check_vma=False,
    )


def solution(mesh):
    dims = (8, 4, 4, 2)
    return build(Mesh(mesh.devices.reshape(dims), AXES), Plan(dims, 512, 1024, 4))
```

time: 188 us -> 91.9 us (0.49)
  blocking collectives: 74.4 us -> 0 us
  Pallas kernels: 101 us -> 79.8 us
    psum x1 -> x0, blocking collectives: 74.4 us -> none  [on_device(): return (group_mean, lax.psum(own, AXES).astype(i32))]
    pallas_call x1, Pallas kernels: 101 us -> 79.8 us  [exchange(): pl.pallas_call(functools.partial(kernel, plan), out_shape=(jax.ShapeDtype...]
where the time goes in v2:
time: 91.9 us; the launch traced here: 91.5 us
  Pallas kernels  79.8 us (87%)
  other arithmetic  5.83 us (6%)
  local copies, waits for them, and re-layouts  3.41 us (4%)
  between operations  2.46 us (3%)
    pallas_call x1, Pallas kernels, exchange(): pl.pallas_call(functools.partial(kernel, plan), out_shape=(jax.ShapeDtype...  79.8 us
    sort x1, other arithmetic, on_device(): lax.sort((place, key_one, second_key), num_keys=1, is_stable=False)  4.98 us
    unnamed x7, local copies, waits for them, and re-layouts  2.9 us

profile of v2, /device:TPU:1, one launch (start us, length us, event | category | flops | bytes accessed | tf_op | source)
XLA Modules:
  0.0 91.5 jit_solution(13574414316713270298)
XLA Ops:
  0.6 0.0 copy-start.1
  0.6 0.7 copy-done.1
  1.3 0.0 copy-start.2
  1.4 0.8 iota_add_fusion
  2.2 0.0 copy-done.2
  2.2 5.0 %sort.21 = (s32[4096]{0:T(1024)S(1)}, s32[4096]{0:T(1024)S(1)}, s32[4096]{0:T(1024)S(1)}) sort(s32[4096]{0:T(1024)S(1)} %get-tuple-element.12, s32[4096]{0:T(1024)S(1)} %get-tuple-element.13, s32[4096]{0:T(1024)S(1)} %copy-done.2), dimensions={0}, to_apply=%region_0.1 | sort | flops 49152 | bytes 98304 | tf_op jit(solution)/shard_map/sort | solution.py:361
  7.2 0.0 copy-start
  7.2 1.2 %copy-done = bf16[4096,128]{1,0:T(8,128)(2,1)S(1)} copy-done((bf16[4096,128]{1,0:T(8,128)(2,1)S(1)}, bf16[4096,128]{1,0:T(8,128)(2,1)}, u32[]{:S(2)}) %copy-start) | copy-done | bytes 1048600
  8.4 79.8 %filter.1 = (bf16[4096,128]{1,0:T(8,128)(2,1)S(1)}, f32[8,128]{1,0:T(8,128)S(1)}) custom-call(bf16[4096,128]{1,0:T(8,128)(2,1)S(1)} %copy-done, s32[32,128]{1,0:T(8,128)S(1)} %fusion.19.ord_ref, s32[32,128]{1,0:T(8,128)S(1)} %bitcast.5, s32[32,128]{1,0:T(8,128)S(1)} %bitcast.6), custom_call_target="tpu_custom_call" | custom-call | tf_op jit(solution)/shard_map/filter/pallas_call | solution.py:324
  88.3 0.5 slice.3
  89.4 1.0 %copy.9 = bf16[4096,128]{1,0:T(8,128)(2,1)} copy(bf16[4096,128]{1,0:T(8,128)(2,1)S(1)} %get-tuple-element.16) | data formatting | bytes 2097152
  (1 shorter events, 0.0 us)
Async XLA Ops:
  0.6 0.7 copy-start.1
  1.3 0.8 copy-start.2
  7.2 1.2 %copy-start = (bf16[4096,128]{1,0:T(8,128)(2,1)S(1)}, bf16[4096,128]{1,0:T(8,128)(2,1)}, u32[]{:S(2)}) copy-start(bf16[4096,128]{1,0:T(8,128)(2,1)} %pay_hbm.1) | copy-start | bytes 3145732

commit v3 on v2

v3 whole, which is shorter than its diff:
```python
import functools

import jax
import jax.numpy as jnp
from jax import lax
from jax.experimental import pallas as pl
from jax.experimental.pallas import tpu as pltpu
from jax.sharding import Mesh
from jax.sharding import PartitionSpec as P

AXES = ("z", "x", "y", "c")
MESH_ID = pl.DeviceIdType.MESH
f32, bf16, i32 = jnp.float32, jnp.bfloat16, jnp.int32
SLOT = 16
LANES = 128


def onehot(mask):
    return jnp.where(mask, 1.0, 0.0).astype(bf16)


def rows_at(start, size, align):
    return pl.ds(pl.multiple_of(start, align), size)


class Plan:
    def __init__(self, dims, block, unrolled=False):
        nz, nx, ny, nc = self.dims = dims
        self.unit = nz * nx
        self.units = ny * nc
        self.devices = self.unit * self.units
        self.rows = self.devices * SLOT
        self.chunk = self.unit * SLOT
        self.block = block
        self.row_lines = self.rows // LANES
        self.unrolled = unrolled
        self.z_steps = [nz // 2]
        for far in range(nz // 2 - 1, 0, -1):
            self.z_steps += [far, nz - far]
        self.z_steps.append(0)

    def loop(self, low, high, body):
        if self.unrolled:
            for i in range(low, high):
                body(i)
        else:
            lax.fori_loop(low, high, lambda i, carry: (body(i), carry)[1], 0)

    def slot_of(self, first_bucket, second_bucket):
        nz, nx, ny, nc = self.dims
        coords = (
            lax.shift_right_logical(first_bucket, nx.bit_length() - 1), first_bucket & (nx - 1),
            lax.shift_right_logical(second_bucket, nc.bit_length() - 1), second_bucket & (nc - 1),
        )
        z, x, y, c = [(at - lax.axis_index(axis)) & (n - 1) for n, axis, at in zip(self.dims, AXES, coords)]
        far = jnp.minimum(z, nz - z)
        z_at = (nz // 2 - 1 - far) * 2 + 1 + jnp.where(z > nz // 2, 1, 0)
        z_at = jnp.where(far == nz // 2, 0, z_at)
        turn = ((y - x) & (ny - 1)) * nc + c
        return (self.units - 1 - turn) * self.unit + z_at * nx + nx - 1 - x


class Partners:
    def __init__(self, plan, sign):
        self.plan, self.sign = plan, sign
        self.me = [lax.axis_index(axis) for axis in AXES]
        self.z = [self.shift(0, step) for step in plan.z_steps]
        self.x = [self.shift(1, step) for step in range(plan.dims[1] - 1, -1, -1)]

    def shift(self, dim, step):
        n = self.plan.dims[dim]
        return lax.rem(self.me[dim] + (step if self.sign > 0 else 2 * n - step), n)

    def each(self, u, act):
        plan = self.plan
        nz, nx, ny, nc = plan.dims
        turn = plan.units - 1 - u
        c = self.shift(3, turn % nc if isinstance(u, int) else lax.rem(turn, nc))
        y_turn = turn // nc if isinstance(u, int) else lax.div(turn, nc)
        y = [self.shift(2, (y_turn + step) % ny if isinstance(u, int) else lax.rem(y_turn + step, ny)) for step in range(nx - 1, -1, -1)]
        for i, z in enumerate(self.z):
            for k, x in enumerate(self.x):
                if isinstance(u, int) and u == plan.units - 1 and i == nz - 1 and k == nx - 1:
                    continue
                act(u * plan.unit + i * nx + k, (z, x, y[k], c))

    def greet(self, barrier):
        plan = self.plan
        nz, nx, ny, nc = plan.dims
        tails = [(self.shift(2, y + ny // 2), self.shift(3, c + 1)) for y in range(ny) for c in range(nc)]
        for i, z in enumerate(self.z):
            for k in range(nx):
                for j, tail in enumerate(tails):
                    own = i == nz - 1 and (k + nx // 2) % nx == 0 and (j // nc + ny // 2) % ny == 0 and (j + 1) % nc == 0
                    if not own:
                        who = (z, self.x[(nx // 2 - 1 - k) % nx], *tail)
                        pl.semaphore_signal(barrier, inc=1, device_id=who, device_id_type=MESH_ID)


def sorted_lines(key, others):
    lines = key.shape[0]
    row, lane = lax.broadcasted_iota(i32, key.shape, 0), lax.broadcasted_iota(i32, key.shape, 1)

    def bit(size):
        at, size = (lane, size) if size < LANES else (row, size // LANES)
        return lax.shift_right_logical(at, size.bit_length() - 1) & 1

    size = 2
    while size <= lines * LANES:
        step = size // 2
        while step:
            upper = bit(step)
            keep_max = upper != bit(size) if size < lines * LANES else upper == 1
            axis, by, span = (1, step, LANES) if step < LANES else (0, step // LANES, lines)

            def other(a, upper=upper, axis=axis, by=by, span=span):
                return jnp.where(upper == 1, pltpu.roll(a, by, axis), pltpu.roll(a, span - by, axis))

            there = other(key)
            new = jnp.where(keep_max, jnp.maximum(key, there), jnp.minimum(key, there))
            moved = new != key
            others = [jnp.where(moved, other(a), a) for a in others]
            key = new
            step //= 2
        size *= 2
    return key, others


def column_form(lines, col_ref, plan):
    turned = jnp.transpose(lines)
    for b in range(plan.row_lines):
        col_ref[pl.ds(b * LANES, LANES), :] = jnp.broadcast_to(turned[:, b : b + 1], (LANES, LANES))


def wide_line(ref, chunk_index, plan):
    n = plan.chunk // LANES
    return jnp.concatenate([ref[pl.ds(chunk_index * n + t, 1), :] for t in range(n)], axis=1)


def kernel(plan, pay_hbm, *refs):
    body(plan, pay_hbm, refs[:3], *refs[3:])


def body(plan, pay_hbm, small, out_ref, dup_ref, fields, ord_ref, pay, send, recv, mean, ret, col_a, col_b,
           tag_send, tag_recv, line_a, line_b, acc, back, near, far, io_sem, tag_sems, pay_send_sem, pay_sems,
           ret_send_sem, ret_sems, dup_sems, field_sems):
    dev, rows, chunk, block = plan.devices, plan.rows, plan.chunk, plan.block
    last_unit = plan.units - 1
    to, source = Partners(plan, 1), Partners(plan, -1)
    loads = [pltpu.make_async_copy(ref, fields.at[i], field_sems.at[i]) for i, ref in enumerate(small)]
    load = pltpu.make_async_copy(pay_hbm, pay, io_sem)
    for each in (*loads, load):
        each.start()
    barrier = pltpu.get_barrier_semaphore()
    to.greet(barrier)

    for each in loads:
        each.wait()
    place, (first_key, second_key) = sorted_lines(fields[0], [fields[1], fields[2]])
    order = place & (rows - 1)
    ord_ref[...] = order
    second_key = pltpu.roll(second_key, LANES // 2, 1)

    part = lax.broadcasted_iota(i32, (8, LANES), 1) // SLOT
    sub = lax.broadcasted_iota(i32, (8, LANES), 0)
    mine = part == sub
    half = part == lax.rem(sub + 4, 8)
    for a in range(plan.row_lines):
        one = jnp.broadcast_to(first_key[a : a + 1, :], (8, LANES))
        two = jnp.broadcast_to(second_key[a : a + 1, :], (8, LANES))
        tag_send[pl.ds(8 * a, 8), :] = jnp.where(mine, one, two)
    column_form(order, col_a, plan)
    load.wait()

    deep = min(1024, rows)
    lane = lax.broadcasted_iota(i32, (chunk, deep), 1)

    def permute(c):
        at = rows_at(c * chunk, chunk, chunk)
        want = jnp.concatenate([col_a[at, :]] * (deep // LANES), axis=1)
        total = jnp.zeros((chunk, LANES), f32)
        for k in range(rows // deep):
            pick = onehot(want - k * deep == lane)
            total = total + jnp.dot(pick, pay[pl.ds(k * deep, deep), :], preferred_element_type=f32)
        send[at, :] = total.astype(bf16)

    def send_tag(slot, who):
        at = pl.ds(slot, 1)
        pltpu.make_async_remote_copy(
            src_ref=tag_send.at[at], dst_ref=tag_recv.at[at], send_sem=tag_sems.at[0], recv_sem=tag_sems.at[1],
            device_id=who, device_id_type=MESH_ID,
        ).start()

    def send_row(slot, who):
        at = rows_at(slot * SLOT, SLOT, SLOT)
        pltpu.make_async_remote_copy(
            src_ref=send.at[at], dst_ref=recv.at[at], send_sem=pay_send_sem,
            recv_sem=pay_sems.at[slot // plan.unit], device_id=who, device_id_type=MESH_ID,
        ).start()

    pl.semaphore_wait(barrier, dev - 1)
    plan.loop(0, plan.units // 2, lambda u: to.each(u, send_tag))
    permute(0)
    plan.loop(plan.units // 2, last_unit, lambda u: to.each(u, send_tag))
    to.each(last_unit, send_tag)
    to.each(0, send_row)
    permute(1)

    def permute_and_send(u):
        permute(u)
        to.each(u - 1, send_row)

    plan.loop(2, plan.units, permute_and_send)
    own = pl.ds(rows - SLOT, SLOT)
    own_line = pl.ds(dev - 1, 1)
    recv[own, :] = send[own, :]
    tag_recv[own_line, :] = tag_send[own_line, :]
    acc[...] = jnp.zeros_like(acc)
    back[...] = jnp.zeros_like(back)
    to.each(last_unit, send_row)

    others = pl.ds(0, dev - 1)
    pltpu.make_async_copy(tag_send.at[others], tag_recv.at[others], tag_sems.at[1]).wait()
    for a in range(plan.row_lines):
        got = tag_recv[pl.ds(8 * a, 8), :]
        line_a[pl.ds(a, 1), :] = jnp.sum(jnp.where(mine, got, 0), axis=0, keepdims=True)
        line_b[pl.ds(a, 1), :] = pltpu.roll(jnp.sum(jnp.where(half, got, 0), axis=0, keepdims=True), LANES // 2, 1)
    column_form(line_a[...], col_a, plan)
    column_form(line_b[...], col_b, plan)
    keys = line_a[...]
    line_a[...] = jnp.where(keys < 0, -2, keys)

    def wait_chunk(src, dst, sems, c, last=False):
        at = pl.ds(0, chunk - SLOT if last else chunk)
        pltpu.make_async_copy(src.at[at], dst.at[at], sems.at[c]).wait()

    def add_pairs(c):
        rhs = jnp.concatenate([recv[rows_at(c * chunk, chunk, chunk), :], jnp.ones((chunk, LANES), bf16)], axis=1)
        one, two = wide_line(line_a, c, plan), wide_line(line_b, c, plan)
        for b in range(rows // block):
            at = pl.ds(b * block, block)
            col_one = jnp.concatenate([col_a[at, :]] * (chunk // LANES), axis=1)
            col_two = jnp.concatenate([col_b[at, :]] * (chunk // LANES), axis=1)
            same = onehot((col_one == one) & (col_two == two))
            acc[at, :] += jnp.dot(same, rhs, preferred_element_type=f32)

    final = last_unit

    def pairs(c):
        wait_chunk(send, recv, pay_sems, c)
        add_pairs(c)

    plan.loop(0, final, pairs)
    wait_chunk(send, recv, pay_sems, final, True)
    add_pairs(final)

    piece = min(256, chunk)
    nz, nx, ny, nc = plan.dims
    plane = nx * ny * nc
    own_near = pl.ds(plane - 1, 1)

    def counts(p, dups):
        at = rows_at(p * piece, piece, piece)
        count = acc[at, pl.ds(LANES, LANES)]
        inverse = 1.0 / jnp.maximum(count, 1.0)
        acc[at, pl.ds(LANES, LANES)] = inverse
        again = jnp.where(count > 0.0, 1.0 - inverse, 0.0)
        return dups + jnp.sum(again.reshape(piece // 8, 8, LANES), axis=0)

    dups = lax.fori_loop(0, rows // piece, counts, jnp.zeros((8, LANES), f32))
    near[own_near, :] = jnp.floor(jnp.sum(dups, axis=0, keepdims=True) + 0.5)

    def finish(p):
        at = rows_at(p * piece, piece, piece)
        mean[at, :] = (acc[at, pl.ds(0, LANES)] * acc[at, pl.ds(LANES, LANES)]).astype(bf16)

    def send_near(step, who):
        pltpu.make_async_remote_copy(
            src_ref=near.at[own_near], dst_ref=near.at[pl.ds(step, 1)], send_sem=dup_sems.at[0],
            recv_sem=dup_sems.at[1], device_id=who, device_id_type=MESH_ID,
        ).start()

    def send_back(slot, who):
        at = rows_at(slot * SLOT, SLOT, SLOT)
        pltpu.make_async_remote_copy(
            src_ref=mean.at[at], dst_ref=ret.at[at], send_sem=ret_send_sem,
            recv_sem=ret_sems.at[slot // plan.unit], device_id=who, device_id_type=MESH_ID,
        ).start()

    pieces = chunk // piece

    def finish_chunk(c):
        for i in range(pieces):
            finish(c * pieces + i)

    def finish_and_send(u):
        finish_chunk(u)
        source.each(u - 1, send_back)

    finish_chunk(0)
    finish_chunk(1)
    for step in range(plane - 1, 0, -1):
        send_near(
            plane - 1 - step, (to.me[0], to.shift(1, step // (ny * nc)), to.shift(2, step // nc % ny), to.shift(3, step % nc))
        )
    source.each(0, send_back)
    plan.loop(2, plan.units, finish_and_send)
    ret[own, :] = mean[own, :]

    near_rows = pl.ds(0, plane - 1)
    pltpu.make_async_copy(near.at[near_rows], near.at[near_rows], dup_sems.at[1]).wait()
    far[pl.ds(0, 1), :] = jnp.sum(near[...], axis=0, keepdims=True)
    source.each(last_unit, send_back)
    for step in range(1, nz):
        pltpu.make_async_remote_copy(
            src_ref=far.at[pl.ds(0, 1)], dst_ref=far.at[pl.ds(step, 1)], send_sem=dup_sems.at[2],
            recv_sem=dup_sems.at[3], device_id=(to.shift(0, step), *to.me[1:]), device_id_type=MESH_ID,
        ).start()

    def add_back(c, last):
        rhs = ret[rows_at(c * chunk, chunk, chunk), :]
        order = wide_line(ord_ref, c, plan)
        own_row = lax.broadcasted_iota(i32, (block, chunk), 0)
        for b in range(rows // block):
            at = pl.ds(b * block, block)
            pick = onehot(own_row == order - b * block)
            total = back[at, :] + jnp.dot(pick, rhs, preferred_element_type=f32)
            if last:
                out_ref[at, :] = total.astype(bf16)
            else:
                back[at, :] = total

    def backs(c):
        wait_chunk(mean, ret, ret_sems, c)
        add_back(c, False)

    plan.loop(0, final, backs)
    far_rows = pl.ds(0, nz - 1)
    pltpu.make_async_copy(far.at[far_rows], far.at[far_rows], dup_sems.at[3]).wait()
    dup_ref[...] = jnp.broadcast_to(jnp.sum(far[...], axis=0, keepdims=True), (8, LANES)).astype(i32)
    wait_chunk(mean, ret, ret_sems, final, True)
    add_back(final, True)
    sent = pl.ds(0, rows - SLOT)
    pltpu.make_async_copy(tag_send.at[others], tag_recv.at[others], tag_sems.at[0]).wait()
    pltpu.make_async_copy(send.at[sent], recv.at[sent], pay_send_sem).wait()
    pltpu.make_async_copy(mean.at[sent], ret.at[sent], ret_send_sem).wait()
    pltpu.make_async_copy(near.at[near_rows], near.at[near_rows], dup_sems.at[0]).wait()
    pltpu.make_async_copy(far.at[far_rows], far.at[far_rows], dup_sems.at[2]).wait()


def on_device(plan, payload, first_key, second_key, live, first_bucket, second_bucket):
    rows, dev, lines = plan.rows, plan.devices, plan.row_lines
    hbm = pl.BlockSpec(memory_space=pltpu.HBM)
    place = plan.slot_of(first_bucket, second_bucket) * rows + lax.iota(i32, rows)
    columns = (place, jnp.where(live > 0, first_key, -1), second_key)
    tile = lambda n, m, t: pltpu.VMEM((n, m), t)
    group_mean, dups = pl.pallas_call(
        functools.partial(kernel, plan),
        out_shape=(jax.ShapeDtypeStruct((rows, LANES), bf16), jax.ShapeDtypeStruct((8, LANES), i32)),
        in_specs=[hbm] * 4,
        out_specs=(pl.BlockSpec(memory_space=pltpu.VMEM),) * 2,
        scratch_shapes=[
            pltpu.VMEM((3, lines, LANES), i32),
            tile(lines, LANES, i32),
            *[tile(rows, LANES, bf16) for _ in range(5)],
            tile(rows, LANES, i32),
            tile(rows, LANES, i32),
            tile(dev, LANES, i32),
            tile(dev, LANES, i32),
            tile(lines, LANES, i32),
            tile(lines, LANES, i32),
            tile(rows, 2 * LANES, f32),
            tile(rows, LANES, f32),
            tile(plan.devices // plan.dims[0], LANES, f32),
            tile(plan.dims[0], LANES, f32),
            pltpu.SemaphoreType.DMA,
            pltpu.SemaphoreType.DMA((2,)),
            pltpu.SemaphoreType.DMA,
            pltpu.SemaphoreType.DMA((plan.units,)),
            pltpu.SemaphoreType.DMA,
            pltpu.SemaphoreType.DMA((plan.units,)),
            pltpu.SemaphoreType.DMA((4,)),
            pltpu.SemaphoreType.DMA((3,)),
        ],
        compiler_params=pltpu.CompilerParams(
            collective_id=0, has_side_effects=True, vmem_limit_bytes=52 * 2**20
        ),
        name="filter",
    )(payload, *[column.reshape(lines, LANES) for column in columns])
    return group_mean, dups[0, 0]


def build(torus, plan):
    rows = P(AXES)
    return jax.shard_map(
        functools.partial(on_device, plan),
        mesh=torus,
        in_specs=(P(AXES, None), rows, rows, rows, rows, rows),
        out_specs=(P(AXES, None), P()),
        check_vma=False,
    )


def solution(mesh):
    dims = (8, 4, 4, 2)
    return build(Mesh(mesh.devices.reshape(dims), AXES), Plan(dims, 1024))
```

time: 91.9 us -> 81 us (0.88)
  other arithmetic: 5.83 us -> 0.8 us
  Pallas kernels: 79.8 us -> 77.1 us
  between operations: 2.46 us -> 0.66 us
  local copies, waits for them, and re-layouts: 3.41 us -> 2.19 us
    sort x1 -> x0, other arithmetic: 4.98 us -> none  [on_device(): lax.sort((place, key_one, second_key), num_keys=1, is_stable=False)]
    pallas_call x1, Pallas kernels: 79.8 us -> 77.1 us  [on_device(): pl.pallas_call(functools.partial(kernel, plan), out_shape=(jax.ShapeDtype...]
    unnamed x7 -> x5, local copies, waits for them, and re-layouts: 2.9 us -> 1.68 us
where the time goes in v3:
time: 81 us; the launch traced here: 80.7 us
  Pallas kernels  77.1 us (95%)
  local copies, waits for them, and re-layouts  2.19 us (3%)
    pallas_call x1, Pallas kernels, on_device(): pl.pallas_call(functools.partial(kernel, plan), out_shape=(jax.ShapeDtype...  77.1 us
    unnamed x5, local copies, waits for them, and re-layouts  1.68 us

profile of v3, /device:TPU:1, one launch (start us, length us, event | category | flops | bytes accessed | tf_op | source)
XLA Modules:
  0.0 80.7 jit_solution(15836099934955127627)
XLA Ops:
  0.6 0.0 copy-start.1
  0.6 0.7 copy-done.1
  1.4 0.0 copy-start
  1.4 0.8 select_bitcast_fusion
  2.1 0.0 copy-done
  2.2 77.1 %filter.1 = (bf16[4096,128]{1,0:T(8,128)(2,1)S(1)}, s32[8,128]{1,0:T(8,128)S(1)}) custom-call(bf16[4096,128]{1,0:T(8,128)(2,1)} %pay_hbm.1, s32[32,128]{1,0:T(8,128)S(1)} %get-tuple-element.7.refs_0_, s32[32,128]{1,0:T(8,128)S(1)} %get-tuple-element.6.refs_1_, s32[32,128]{1,0:T(8,128)S(1)} %bitcast.6), custom_call_target="tpu_custom_call" | custom-call | tf_op jit(solution)/shard_map/filter/pallas_call | solution.py:357
  79.3 0.5 slice.3
  79.8 1.0 %copy.9 = bf16[4096,128]{1,0:T(8,128)(2,1)} copy(bf16[4096,128]{1,0:T(8,128)(2,1)S(1)} %get-tuple-element.10) | data formatting | bytes 2097152
Async XLA Ops:
  0.6 0.7 copy-start.1
  1.4 0.8 copy-start

commit v4 on v3

--- a/solution.py
+++ b/solution.py
@@ -17,6 +17,13 @@
 
 def onehot(mask):
     return jnp.where(mask, 1.0, 0.0).astype(bf16)
+
+
+def when(condition, act):
+    if not isinstance(condition, bool):
+        pl.when(condition)(act)
+    elif condition:
+        act()
 
 
 def rows_at(start, size, align):
@@ -142,7 +149,7 @@
 
 
 def body(plan, pay_hbm, small, out_ref, dup_ref, fields, ord_ref, pay, send, recv, mean, ret, col_a, col_b,
-           tag_send, tag_recv, line_a, line_b, acc, back, near, far, io_sem, tag_sems, pay_send_sem, pay_sems,
+           tag_send, tag_recv, tag_other, line_a, line_b, acc, back, near, far, io_sem, tag_sems, pay_send_sem, pay_sems,
            ret_send_sem, ret_sems, dup_sems, field_sems):
     dev, rows, chunk, block = plan.devices, plan.rows, plan.chunk, plan.block
     last_unit = plan.units - 1
@@ -163,12 +170,19 @@
 
     part = lax.broadcasted_iota(i32, (8, LANES), 1) // SLOT
     sub = lax.broadcasted_iota(i32, (8, LANES), 0)
-    mine = part == sub
-    half = part == lax.rem(sub + 4, 8)
-    for a in range(plan.row_lines):
-        one = jnp.broadcast_to(first_key[a : a + 1, :], (8, LANES))
-        two = jnp.broadcast_to(second_key[a : a + 1, :], (8, LANES))
-        tag_send[pl.ds(8 * a, 8), :] = jnp.where(mine, one, two)
+    spots = [part == lax.rem(sub + q, 8) for q in (0, 4, 2, 6)]
+    quarter = LANES // 4
+    tagged = [first_key, second_key, pltpu.roll(first_key, quarter, 1), pltpu.roll(second_key, quarter, 1)]
+    unit_lines = plan.unit // 8
+    pairs_of_units = plan.units // 2
+    for v in range(pairs_of_units):
+        for i in range(unit_lines):
+            other, like = 2 * v * unit_lines + i, (2 * v + 1) * unit_lines + i
+            one, two, three, four = [
+                jnp.broadcast_to(keys[at : at + 1, :], (8, LANES)) for keys, at in zip(tagged, (like, like, other, other))
+            ]
+            line = jnp.where(spots[0], one, jnp.where(spots[1], two, jnp.where(spots[2], three, four)))
+            tag_send[pl.ds(v * plan.unit + 8 * i, 8), :] = line
     column_form(order, col_a, plan)
     load.wait()
 
@@ -184,12 +198,15 @@
             total = total + jnp.dot(pick, pay[pl.ds(k * deep, deep), :], preferred_element_type=f32)
         send[at, :] = total.astype(bf16)
 
-    def send_tag(slot, who):
-        at = pl.ds(slot, 1)
-        pltpu.make_async_remote_copy(
-            src_ref=tag_send.at[at], dst_ref=tag_recv.at[at], send_sem=tag_sems.at[0], recv_sem=tag_sems.at[1],
-            device_id=who, device_id_type=MESH_ID,
-        ).start()
+    def send_tags(v):
+        def send_tag(slot, who):
+            at = pl.ds(slot - plan.unit * (v + 1), 1)
+            pltpu.make_async_remote_copy(
+                src_ref=tag_send.at[at], dst_ref=tag_recv.at[at], send_sem=tag_sems.at[0], recv_sem=tag_sems.at[1],
+                device_id=who, device_id_type=MESH_ID,
+            ).start()
+
+        to.each(2 * v + 1, send_tag)
 
     def send_row(slot, who):
         at = rows_at(slot * SLOT, SLOT, SLOT)
@@ -199,32 +216,47 @@
         ).start()
 
     pl.semaphore_wait(barrier, dev - 1)
-    plan.loop(0, plan.units // 2, lambda u: to.each(u, send_tag))
-    permute(0)
-    plan.loop(plan.units // 2, last_unit, lambda u: to.each(u, send_tag))
-    to.each(last_unit, send_tag)
-    to.each(0, send_row)
-    permute(1)
+    plan.loop(0, pairs_of_units // 2, send_tags)
+
+    def first_sent():
+        plan.loop(pairs_of_units // 2, pairs_of_units - 1, send_tags)
+        send_tags(pairs_of_units - 1)
+        to.each(0, send_row)
 
     def permute_and_send(u):
         permute(u)
-        to.each(u - 1, send_row)
-
-    plan.loop(2, plan.units, permute_and_send)
+        when(u == 0, first_sent)
+        when(u >= 2, lambda: to.each(u - 1, send_row))
+
+    plan.loop(0, plan.units, permute_and_send)
+    lines = dev // 2
+    others, own_line = pl.ds(0, lines - 1), pl.ds(lines - 1, 1)
+    tag_recv[own_line, :] = tag_send[own_line, :]
     own = pl.ds(rows - SLOT, SLOT)
-    own_line = pl.ds(dev - 1, 1)
     recv[own, :] = send[own, :]
-    tag_recv[own_line, :] = tag_send[own_line, :]
+    pltpu.make_async_copy(tag_send.at[others], tag_recv.at[others], tag_sems.at[1]).wait()
+    forward = pltpu.make_async_remote_copy(
+        src_ref=tag_recv, dst_ref=tag_other, send_sem=tag_sems.at[2], recv_sem=tag_sems.at[3],
+        device_id=(*to.me[:3], to.shift(3, 1)), device_id_type=MESH_ID,
+    )
+    to.each(last_unit, send_row)
+    forward.start()
     acc[...] = jnp.zeros_like(acc)
     back[...] = jnp.zeros_like(back)
-    to.each(last_unit, send_row)
-
-    others = pl.ds(0, dev - 1)
-    pltpu.make_async_copy(tag_send.at[others], tag_recv.at[others], tag_sems.at[1]).wait()
-    for a in range(plan.row_lines):
-        got = tag_recv[pl.ds(8 * a, 8), :]
-        line_a[pl.ds(a, 1), :] = jnp.sum(jnp.where(mine, got, 0), axis=0, keepdims=True)
-        line_b[pl.ds(a, 1), :] = pltpu.roll(jnp.sum(jnp.where(half, got, 0), axis=0, keepdims=True), LANES // 2, 1)
+
+    def take(ref, v, i, line, at, by):
+        got = ref[pl.ds(v * plan.unit + 8 * i, 8), :]
+        one, two = [jnp.sum(jnp.where(spot, got, 0), axis=0, keepdims=True) for spot in spots[at : at + 2]]
+        line_a[pl.ds(line, 1), :] = pltpu.roll(one, by, 1) if by else one
+        line_b[pl.ds(line, 1), :] = pltpu.roll(two, (LANES // 2 + by) % LANES, 1)
+
+    for v in range(pairs_of_units):
+        for i in range(unit_lines):
+            take(tag_recv, v, i, (2 * v + 1) * unit_lines + i, 0, 0)
+    forward.wait_recv()
+    for v in range(pairs_of_units):
+        for i in range(unit_lines):
+            take(tag_other, v, i, 2 * v * unit_lines + i, 2, LANES - quarter)
     column_form(line_a[...], col_a, plan)
     column_form(line_b[...], col_b, plan)
     keys = line_a[...]
@@ -342,6 +374,7 @@
     add_back(final, True)
     sent = pl.ds(0, rows - SLOT)
     pltpu.make_async_copy(tag_send.at[others], tag_recv.at[others], tag_sems.at[0]).wait()
+    forward.wait_send()
     pltpu.make_async_copy(send.at[sent], recv.at[sent], pay_send_sem).wait()
     pltpu.make_async_copy(mean.at[sent], ret.at[sent], ret_send_sem).wait()
     pltpu.make_async_copy(near.at[near_rows], near.at[near_rows], dup_sems.at[0]).wait()
@@ -365,8 +398,7 @@
             *[tile(rows, LANES, bf16) for _ in range(5)],
             tile(rows, LANES, i32),
             tile(rows, LANES, i32),
-            tile(dev, LANES, i32),
-            tile(dev, LANES, i32),
+            *[tile(dev // 2, LANES, i32) for _ in range(3)],
             tile(lines, LANES, i32),
             tile(lines, LANES, i32),
             tile(rows, 2 * LANES, f32),
@@ -374,7 +406,7 @@
             tile(plan.devices // plan.dims[0], LANES, f32),
             tile(plan.dims[0], LANES, f32),
             pltpu.SemaphoreType.DMA,
-            pltpu.SemaphoreType.DMA((2,)),
+            pltpu.SemaphoreType.DMA((4,)),
             pltpu.SemaphoreType.DMA,
             pltpu.SemaphoreType.DMA((plan.units,)),
             pltpu.SemaphoreType.DMA,

time: 81 us -> 78.4 us (0.968)
  Pallas kernels: 77.1 us -> 74.5 us
    pallas_call x1, Pallas kernels: 77.1 us -> 74.5 us  [on_device(): pl.pallas_call(functools.partial(kernel, plan), out_shape=(jax.ShapeDtype...]
where the time goes in v4:
time: 78.4 us; the launch traced here: 78.1 us
  Pallas kernels  74.5 us (95%)
  local copies, waits for them, and re-layouts  2.19 us (3%)
  other arithmetic  0.8 us (1%)
    pallas_call x1, Pallas kernels, on_device(): pl.pallas_call(functools.partial(kernel, plan), out_shape=(jax.ShapeDtype...  74.5 us
    unnamed x5, local copies, waits for them, and re-layouts  1.68 us

profile of v4, /device:TPU:1, one launch (start us, length us, event | category | flops | bytes accessed | tf_op | source)
XLA Modules:
  0.0 78.1 jit_solution(2742049239495410049)
XLA Ops:
  0.6 0.0 copy-start.1
  0.6 0.7 copy-done.1
  1.4 0.0 copy-start
  1.4 0.8 %select_bitcast_fusion = (s32[32,128]{1,0:T(8,128)S(1)}, s32[32,128]{1,0:T(8,128)S(1)}) fusion(s32[4096]{0:T(1024)S(1)} %copy-done.1, s32[4096]{0:T(1024)} %param.9, s32[]{:T(128)S(6)} %axis_index.51, s32[4096]{0:T(1024)} %param.10, s32[]{:T(128)S(6)} %axis_index.48, s32[4096]{0:T(1024)} %param.11, s32[]{:T(128)S(6)} %axis_index.46, s32[]{:T(128)S(6)} %axis_index.43), kind=kLoop, calls=%fused_computation.1 | loop fusion | flops 147456 | bytes 98320 | tf_op jit(solution)/shard_map/reshape | solution.py:421
  2.1 0.0 copy-done
  2.2 74.5 %filter.1 = (bf16[4096,128]{1,0:T(8,128)(2,1)S(1)}, s32[8,128]{1,0:T(8,128)S(1)}) custom-call(bf16[4096,128]{1,0:T(8,128)(2,1)} %pay_hbm.1, s32[32,128]{1,0:T(8,128)S(1)} %get-tuple-element.7.refs_0_, s32[32,128]{1,0:T(8,128)S(1)} %get-tuple-element.6.refs_1_, s32[32,128]{1,0:T(8,128)S(1)} %bitcast.6), custom_call_target="tpu_custom_call" | custom-call | tf_op jit(solution)/shard_map/filter/pallas_call | solution.py:390
  76.7 0.5 slice.3
  77.2 1.0 %copy.9 = bf16[4096,128]{1,0:T(8,128)(2,1)} copy(bf16[4096,128]{1,0:T(8,128)(2,1)S(1)} %get-tuple-element.10) | data formatting | bytes 2097152
Async XLA Ops:
  0.6 0.7 copy-start.1
  1.4 0.8 %copy-start = (s32[4096]{0:T(1024)S(1)}, s32[4096]{0:T(1024)}, u32[]{:S(2)}) copy-start(s32[4096]{0:T(1024)} %param.8) | copy-start | bytes 49156

commit v5 on v4

--- a/solution.py
+++ b/solution.py
@@ -218,6 +218,18 @@
     pl.semaphore_wait(barrier, dev - 1)
     plan.loop(0, pairs_of_units // 2, send_tags)
 
+    lines = dev // 2
+    others, own_line = pl.ds(0, lines - 1), pl.ds(lines - 1, 1)
+    tag_recv[own_line, :] = tag_send[own_line, :]
+    forward = pltpu.make_async_remote_copy(
+        src_ref=tag_recv, dst_ref=tag_other, send_sem=tag_sems.at[2], recv_sem=tag_sems.at[3],
+        device_id=(*to.me[:3], to.shift(3, 1)), device_id_type=MESH_ID,
+    )
+
+    def hand_on():
+        pltpu.make_async_copy(tag_send.at[others], tag_recv.at[others], tag_sems.at[1]).wait()
+        forward.start()
+
     def first_sent():
         plan.loop(pairs_of_units // 2, pairs_of_units - 1, send_tags)
         send_tags(pairs_of_units - 1)
@@ -227,22 +239,13 @@
         permute(u)
         when(u == 0, first_sent)
         when(u >= 2, lambda: to.each(u - 1, send_row))
+        when(u == last_unit - 1, hand_on)
 
     plan.loop(0, plan.units, permute_and_send)
-    lines = dev // 2
-    others, own_line = pl.ds(0, lines - 1), pl.ds(lines - 1, 1)
-    tag_recv[own_line, :] = tag_send[own_line, :]
     own = pl.ds(rows - SLOT, SLOT)
     recv[own, :] = send[own, :]
-    pltpu.make_async_copy(tag_send.at[others], tag_recv.at[others], tag_sems.at[1]).wait()
-    forward = pltpu.make_async_remote_copy(
-        src_ref=tag_recv, dst_ref=tag_other, send_sem=tag_sems.at[2], recv_sem=tag_sems.at[3],
-        device_id=(*to.me[:3], to.shift(3, 1)), device_id_type=MESH_ID,
-    )
     to.each(last_unit, send_row)
-    forward.start()
     acc[...] = jnp.zeros_like(acc)
-    back[...] = jnp.zeros_like(back)
 
     def take(ref, v, i, line, at, by):
         got = ref[pl.ds(v * plan.unit + 8 * i, 8), :]
@@ -366,6 +369,7 @@
         wait_chunk(mean, ret, ret_sems, c)
         add_back(c, False)
 
+    back[...] = jnp.zeros_like(back)
     plan.loop(0, final, backs)
     far_rows = pl.ds(0, nz - 1)
     pltpu.make_async_copy(far.at[far_rows], far.at[far_rows], dup_sems.at[3]).wait()

time: 78.4 us -> 77.9 us (level)
  no operation moved by 1% of the time
where the time goes in v5:
time: 77.9 us; the launch traced here: 77.7 us
  Pallas kernels  74 us (95%)
  local copies, waits for them, and re-layouts  2.19 us (3%)
  other arithmetic  0.8 us (1%)
    pallas_call x1, Pallas kernels, on_device(): pl.pallas_call(functools.partial(kernel, plan), out_shape=(jax.ShapeDtype...  74 us
    unnamed x5, local copies, waits for them, and re-layouts  1.68 us

profile of v5, /device:TPU:1, one launch (start us, length us, event | category | flops | bytes accessed | tf_op | source)
XLA Modules:
  0.0 77.7 jit_solution(3975053506271884309)
XLA Ops:
  0.6 0.0 copy-start.1
  0.6 0.7 copy-done.1
  1.4 0.0 copy-start
  1.4 0.8 %select_bitcast_fusion = (s32[32,128]{1,0:T(8,128)S(1)}, s32[32,128]{1,0:T(8,128)S(1)}) fusion(s32[4096]{0:T(1024)S(1)} %copy-done.1, s32[4096]{0:T(1024)} %param.9, s32[]{:T(128)S(6)} %axis_index.51, s32[4096]{0:T(1024)} %param.10, s32[]{:T(128)S(6)} %axis_index.48, s32[4096]{0:T(1024)} %param.11, s32[]{:T(128)S(6)} %axis_index.46, s32[]{:T(128)S(6)} %axis_index.43), kind=kLoop, calls=%fused_computation.1 | loop fusion | flops 147456 | bytes 98320 | tf_op jit(solution)/shard_map/reshape | solution.py:425
  2.1 0.0 copy-done
  2.2 74.0 %filter.1 = (bf16[4096,128]{1,0:T(8,128)(2,1)S(1)}, s32[8,128]{1,0:T(8,128)S(1)}) custom-call(bf16[4096,128]{1,0:T(8,128)(2,1)} %pay_hbm.1, s32[32,128]{1,0:T(8,128)S(1)} %get-tuple-element.7.refs_0_, s32[32,128]{1,0:T(8,128)S(1)} %get-tuple-element.6.refs_1_, s32[32,128]{1,0:T(8,128)S(1)} %bitcast.6), custom_call_target="tpu_custom_call" | custom-call | tf_op jit(solution)/shard_map/filter/pallas_call | solution.py:394
  76.2 0.5 slice.3
  76.7 1.0 %copy.9 = bf16[4096,128]{1,0:T(8,128)(2,1)} copy(bf16[4096,128]{1,0:T(8,128)(2,1)S(1)} %get-tuple-element.10) | data formatting | bytes 2097152
Async XLA Ops:
  0.6 0.7 copy-start.1
  1.4 0.8 %copy-start = (s32[4096]{0:T(1024)S(1)}, s32[4096]{0:T(1024)}, u32[]{:S(2)}) copy-start(s32[4096]{0:T(1024)} %param.8) | copy-start | bytes 49156
